TPU v7x, 256 devices: a whole 4x4x8 slice. The times are simulated.
256 devices in a mesh: seq: 32 (over y, z), mp: 8 (over x, core).
Axes of the slice: x: 4, y: 4, z: 8, core: 2. Of those that a mesh axis runs over, the one named last changes fastest.
Arguments:
- tokens: bfloat16 [12288, 2048], P('seq'), may hold values from -24 to 24
- database: bfloat16 [256, 96, 896], P('seq'), may hold values from -24 to 24
- nb_shard: int32 [192, 2], replicated, may hold values from 0 to 31, all different within a row; in each aligned block of 6 rows (0 to 5, 6 to 11, ...) no two rows name the same one
- nb_row: int32 [192, 2], replicated, may hold values from 0 to 7
- dec_gain: float32 [2048], replicated, may hold values from 0.1 to 1.9
- enc_gain: float32 [896], replicated, may hold values from 0.1 to 1.9
- w_in: bfloat16 [896, 1792], replicated, may hold values from -0.1875 to 0.1875
- w_out: bfloat16 [1792, 896], replicated, may hold values from -0.125 to 0.125
- w_query: bfloat16 [2048, 2048], P(None, 'mp'), may hold values from -0.125 to 0.125
- w_key: bfloat16 [896, 2048], P(None, 'mp'), may hold values from -0.1875 to 0.1875
- w_value: bfloat16 [896, 2048], P(None, 'mp'), may hold values from -0.1875 to 0.1875
- w_proj: bfloat16 [2048, 2048], P('mp'), may hold values from -0.5 to 0.5
- grad_out: bfloat16 [12288, 2048], P('seq'), may hold values from -6 to 6
Outputs:
- cca: bfloat16 [12288, 2048], P('seq', 'mp')
- grad_tokens: float32 [12288, 2048], P('seq', 'mp')
- grad_database: float32 [256, 96, 896], P('seq', 'mp')
Inputs may be any that keep to these rules, and one draw needn't show every extreme that they name: `nb_shard`: in each aligned block of 6 stretches (the stretches of one device) no shard is named more than 1 times, and some block reaches it; the 2 neighbours of a stretch come from different shards.
All inputs are finite; a program needn't handle non-finite values.
Results may differ from a plain program's by a relative error of at most 0.017.
Values may be sent and summed in bfloat16 or wider, within the bound.
A program may use at most 128 MiB of HBM per device.

v0:
```python
import jax
import jax.numpy as jnp
from jax import lax
from jax.sharding import Mesh
from jax.sharding import PartitionSpec as P

HD = 128
L = 96
STRETCH = 64
K = 2
SEQ_LEN = 4096
MP = ("mp_0", "mp_1")


EPSILON = 1e-06


def cut_rows(length, count):
    unit = 8 if length >= 8 * count else 1
    return [length // unit * k // count * unit for k in range(1, count)]


def gather_in_order(x, axes, sequence):
    tiles = x[None]
    for k in sequence:
        tiles = lax.all_gather(tiles, axes[k], axis=0, tiled=True)
    block = [lax.axis_size(axes[k]) for k in reversed(sequence)]
    tiles = tiles.reshape(*block, *x.shape)
    turned = sorted(range(len(sequence)), key=lambda place: sequence[len(sequence) - 1 - place])
    return tiles.transpose(*turned, *range(len(sequence), tiles.ndim)).reshape(-1, *x.shape)


def joined_along(tiles, dim):
    shape = list(tiles.shape[1:])
    shape[dim] *= tiles.shape[0]
    return jnp.moveaxis(tiles, 0, dim).reshape(shape)


def spread_gather(x, axes, dim):
    widest = max(range(max(1, x.ndim - 1)), key=lambda d: x.shape[d])
    count, outs = (len(axes), [])
    for leading, section in enumerate(jnp.split(x, cut_rows(x.shape[widest], count), axis=widest)):
        if section.size:
            sequence = [(leading - k) % count for k in range(count)]
            outs.append(gather_in_order(section, axes, sequence))
    return joined_along(jnp.concatenate(outs, axis=widest + 1), dim)


def split_up(x, dim, devices):
    shape = x.shape
    tiles = x.reshape(*shape[:dim], devices, shape[dim] // devices, *shape[dim + 1 :])
    return jnp.moveaxis(tiles, dim, 0)


def summed_on_arrival(x, axis, dim):
    devices = lax.axis_size(axis)
    tiles = lax.all_to_all(split_up(x, dim, devices), axis, 0, 0, tiled=True)
    return jnp.sum(tiles.astype(jnp.float32), axis=0)


def in_one_piece(arrays, axis, dim, along):
    both = jnp.concatenate(arrays, axis=along)
    out, at, outs = (lax.psum_scatter(both, axis, scatter_dimension=dim, tiled=True), 0, [])
    for a in arrays:
        outs.append(lax.slice_in_dim(out, at, at + a.shape[along], axis=along))
        at += a.shape[along]
    return tuple(outs)


def rms_scaling(values):
    return lax.rsqrt(jnp.mean(values * values, axis=-1, keepdims=True) + EPSILON)


def silu_slope(pre_act):
    sigmoid = jax.nn.sigmoid(pre_act)
    return sigmoid * (1.0 + pre_act * (1.0 - sigmoid))


def dot_t(matrix, weight):
    return lax.dot_general(
        matrix, weight, (((1,), (1,)), ((), ())), preferred_element_type=jnp.float32
    )


def encode(embedded, enc_gain, w_in, w_out):
    values = embedded.astype(jnp.float32)
    scaling = rms_scaling(values)
    normed = (values * scaling * enc_gain).astype(jnp.bfloat16)
    pre_act = jnp.einsum("nle,ef->nlf", normed, w_in, preferred_element_type=jnp.float32)
    hidden = jax.nn.silu(pre_act).astype(jnp.bfloat16)
    mixed = jnp.einsum("nlf,fe->nle", hidden, w_out, preferred_element_type=jnp.float32)
    encoded = (values + mixed).astype(jnp.bfloat16)
    return (encoded, pre_act, scaling)


def encode_back(embedded, pre_act, scaling, grad_enc, enc_gain, w_in, w_out):
    grad_hidden = jnp.einsum(
        "nle,fe->nlf", grad_enc.astype(jnp.bfloat16), w_out, preferred_element_type=jnp.float32
    )
    grad_pre = (grad_hidden * silu_slope(pre_act)).astype(jnp.bfloat16)
    grad_unit = (
        jnp.einsum("nlf,ef->nle", grad_pre, w_in, preferred_element_type=jnp.float32) * enc_gain
    )
    unit_rows = embedded.astype(jnp.float32) * scaling
    return grad_enc + scaling * (
        grad_unit - unit_rows * jnp.mean(grad_unit * unit_rows, axis=-1, keepdims=True)
    )


def body(
    tokens,
    database,
    nb_shard,
    nb_row,
    dec_gain,
    enc_gain,
    w_in,
    w_out,
    w_query,
    w_key,
    w_value,
    w_proj,
    grad_out,
):
    seq_count = lax.axis_size("seq")
    my_seq = lax.axis_index("seq")
    mp_count = lax.axis_size(MP)
    my_mp = lax.axis_index(MP)
    tok_rows = tokens.shape[0]
    stretches_here = tok_rows // STRETCH
    width = w_query.shape[1]
    heads_here = width // HD
    nb_here = stretches_here * K
    slot_cap = max(1, (nb_here + seq_count - 1) // seq_count)
    slot_count = seq_count * slot_cap
    tok_span = database.shape[1] // mp_count
    tok_start = my_mp * tok_span
    requests = nb_shard.reshape(seq_count, nb_here)
    req_rows = nb_row.reshape(seq_count, nb_here)
    req_order = jnp.arange(nb_here)
    same_shard = requests[:, :, None] == requests[:, None, :]
    before = req_order[None, :] < req_order[:, None]
    slot_rank = jnp.sum((same_shard & before[None]).astype(jnp.int32), axis=2)
    held_here = requests == my_seq
    slot_ids = jnp.arange(slot_cap)
    slot_pick = held_here[:, None, :] & (slot_rank[:, None, :] == slot_ids[None, :, None])
    slot_row = jnp.sum(slot_pick.astype(jnp.int32) * req_rows[:, None, :], axis=2).reshape(
        slot_count
    )
    slot_live = jnp.any(slot_pick, axis=2).reshape(slot_count)
    own_req = lax.dynamic_index_in_dim(requests, my_seq, 0, keepdims=False)
    own_rank = lax.dynamic_index_in_dim(slot_rank, my_seq, 0, keepdims=False)
    source = own_req * slot_cap + own_rank
    kv_weight = jnp.concatenate([w_key, w_value], axis=1)
    own_slice = lax.dynamic_slice_in_dim(database, tok_start, tok_span, 1)
    outgoing = jnp.take(own_slice, slot_row, axis=0)
    arrived = lax.all_to_all(outgoing, "seq", split_axis=0, concat_axis=0, tiled=True)
    embed_part = jnp.take(arrived, source, axis=0)
    enc_part, pre_part, scale_part = encode(embed_part, enc_gain, w_in, w_out)
    kv_rows = jnp.einsum(
        "nle,ef->nlf", spread_gather(enc_part, MP, 1), kv_weight, preferred_element_type=jnp.float32
    ).astype(jnp.bfloat16)
    key_rows = kv_rows[:, :, :width]
    value_rows = kv_rows[:, :, width:]
    tok_vals = tokens.astype(jnp.float32)
    tok_scaling = rms_scaling(tok_vals)
    tok_unit = tok_vals * tok_scaling
    tok_normed = (tok_unit * dec_gain).astype(jnp.bfloat16)
    query_rows = jnp.dot(tok_normed, w_query, preferred_element_type=jnp.float32).astype(
        jnp.bfloat16
    )
    query_blk = query_rows.reshape(stretches_here, STRETCH, heads_here, HD)
    key_blk = key_rows.reshape(stretches_here, K * L, heads_here, HD)
    value_blk = value_rows.reshape(stretches_here, K * L, heads_here, HD)
    factor = HD ** (-0.5)
    scores = (
        jnp.einsum("cqhd,ckhd->chqk", query_blk, key_blk, preferred_element_type=jnp.float32)
        * factor
    )
    exp_score = jnp.exp(scores)
    attn_prob = exp_score / jnp.sum(exp_score, axis=-1, keepdims=True)
    attn_weight = attn_prob.astype(jnp.bfloat16)
    context = (
        jnp.einsum("chqk,ckhd->cqhd", attn_weight, value_blk, preferred_element_type=jnp.float32)
        .astype(jnp.bfloat16)
        .reshape(tok_rows, width)
    )
    stretch_pos = (my_seq * stretches_here + jnp.arange(stretches_here)) % (SEQ_LEN // STRETCH)
    live_tok = jnp.repeat(stretch_pos != 0, STRETCH)[:, None]
    out_terms = jnp.where(
        live_tok, jnp.dot(context, w_proj, preferred_element_type=jnp.float32), 0.0
    )
    masked = jnp.where(live_tok, grad_out, jnp.zeros_like(grad_out))
    grad_ctx = dot_t(masked, w_proj).astype(jnp.bfloat16)
    grad_blk = grad_ctx.reshape(stretches_here, STRETCH, heads_here, HD)
    grad_prob = jnp.einsum(
        "cqhd,ckhd->chqk", grad_blk, value_blk, preferred_element_type=jnp.float32
    )
    grad_score = (
        attn_prob * (grad_prob - jnp.sum(attn_prob * grad_prob, axis=-1, keepdims=True)) * factor
    ).astype(jnp.bfloat16)
    grad_value = jnp.einsum(
        "chqk,cqhd->ckhd", attn_weight, grad_blk, preferred_element_type=jnp.float32
    ).astype(jnp.bfloat16)
    grad_query = (
        jnp.einsum("chqk,ckhd->cqhd", grad_score, key_blk, preferred_element_type=jnp.float32)
        .astype(jnp.bfloat16)
        .reshape(tok_rows, width)
    )
    grad_key = jnp.einsum(
        "chqk,cqhd->ckhd", grad_score, query_blk, preferred_element_type=jnp.float32
    ).astype(jnp.bfloat16)
    key_grad = grad_key.reshape(nb_here, L, width)
    value_grad = grad_value.reshape(nb_here, L, width)
    enc_terms = jnp.einsum("nlf,ef->nle", key_grad, w_key, preferred_element_type=jnp.float32)
    enc_terms = enc_terms + jnp.einsum(
        "nlf,ef->nle", value_grad, w_value, preferred_element_type=jnp.float32
    )
    grad_enc = summed_on_arrival(enc_terms.astype(jnp.bfloat16), MP, 1)
    grad_normed = dot_t(grad_query, w_query)
    tok_grad = grad_normed * dec_gain
    tok_terms = tok_scaling * (
        tok_grad - tok_unit * jnp.mean(tok_grad * tok_unit, axis=-1, keepdims=True)
    )
    grad_embed = encode_back(embed_part, pre_part, scale_part, grad_enc, enc_gain, w_in, w_out)
    place_back = (source[:, None] == jnp.arange(slot_count)[None, :]).astype(jnp.float32)
    returned = jnp.einsum("ns,nle->sle", place_back, grad_embed, precision=lax.Precision.HIGHEST)
    received = lax.all_to_all(
        returned.astype(jnp.bfloat16), "seq", split_axis=0, concat_axis=0, tiled=True
    ).astype(returned.dtype)
    row_hit = (
        (slot_row[None, :] == jnp.arange(database.shape[0])[:, None]) & slot_live[None, :]
    ).astype(jnp.float32)
    grad_database = jnp.einsum("rs,sle->rle", row_hit, received, precision=lax.Precision.HIGHEST)
    cca_sum, grad_sum = tuple(
        (
            part.astype(jnp.float32)
            for part in in_one_piece(
                (out_terms.astype(jnp.bfloat16), tok_terms.astype(jnp.bfloat16)), MP, 1, 0
            )
        )
    )
    return (cca_sum.astype(jnp.bfloat16), grad_sum, grad_database)


def solution(mesh):
    split = Mesh(mesh.devices.reshape(mesh.shape["seq"], 4, 2), ("seq", "mp_0", "mp_1"))
    placed = (
        P("seq", None),
        P("seq", None, None),
        P(),
        P(),
        P(),
        P(),
        P(),
        P(),
        P(None, MP),
        P(None, MP),
        P(None, MP),
        P(MP, None),
        P("seq", None),
    )
    return jax.shard_map(
        body,
        mesh=split,
        in_specs=placed,
        out_specs=(P("seq", MP), P("seq", MP), P("seq", MP, None)),
        check_vma=False,
    )
```

profile of v0, /device:TPU:1, one launch (start us, length us, event | category | flops | bytes accessed | tf_op | source)
XLA Modules:
  0.0 248.1 jit_solution(8221677842646894722)
XLA Ops:
  7.2 0.9 copy.90
  11.6 1.0 constant_dynamic-slice_fusion
  12.7 1.6 gather_fusion
  14.3 2.3 broadcast_select_fusion
  16.6 12.3 %all-to-all-start = ((bf16[32,12,896]{2,1,0:T(8,128)(2,1)}), bf16[32,12,896]{2,1,0:T(8,128)(2,1)}, u32[]{:S(2)}, u32[]{:S(2)}) async-start(bf16[32,12,896]{2,1,0:T(8,128)(2,1)} %broadcast_select_fusion), calls=%async_computation | async-start | bytes 1835008 | tf_op jit(solution)/shard_map/all_to_all | solution.py:157
  29.1 1.8 fusion.17
  31.0 2.3 fusion.47
  34.0 2.3 fusion.50
  38.4 12.6 %all-to-all-done = bf16[32,12,896]{2,1,0:T(8,128)(2,1)} async-done(((bf16[32,12,896]{2,1,0:T(8,128)(2,1)}), bf16[32,12,896]{2,1,0:T(8,128)(2,1)}, u32[]{:S(2)}, u32[]{:S(2)}) %all-to-all-start) | async-done | bytes 688160 | tf_op jit(solution)/shard_map/all_to_all | solution.py:157
  51.1 1.9 gather_fusion.1
  54.5 1.8 fusion.10
  56.4 0.9 fusion.44
  57.6 6.5 %all-gather.1 = bf16[12,12,896]{2,1,0:T(8,128)(2,1)S(1)} all-gather(bf16[6,12,896]{2,1,0:T(8,128)(2,1)S(1)} %get-tuple-element.10), channel_id=3, replica_groups=mesh['seq'=32,'mp_0'=4,'mp_1'=2] {'mp_1'}, dimensions={0}, use_global_device_ids=true | all-gather | bytes 387072 | tf_op jit(solution)/shard_map/all_gather | solution.py:26
  64.1 11.6 %all-gather = bf16[24,12,896]{2,1,0:T(8,128)(2,1)S(1)} all-gather(bf16[6,12,896]{2,1,0:T(8,128)(2,1)S(1)} %get-tuple-element.9), channel_id=2, replica_groups=mesh['seq'=32,'mp_0'=4,'mp_1'=2] {'mp_0'}, dimensions={0}, use_global_device_ids=true | all-gather | bytes 645120 | tf_op jit(solution)/shard_map/all_gather | solution.py:26
  75.7 4.7 %all_gather.13 = bf16[8,6,12,896]{3,2,1,0:T(8,128)(2,1)S(1)} all-gather(bf16[4,6,12,896]{3,2,1,0:T(8,128)(2,1)S(1)} %bitcast.93), channel_id=1, replica_groups=mesh['seq'=32,'mp_0'=4,'mp_1'=2] {'mp_1'}, dimensions={0}, use_global_device_ids=true | all-gather | bytes 1548288 | tf_op jit(solution)/shard_map/all_gather | solution.py:26
  80.6 15.7 %all_gather.15 = bf16[8,6,12,896]{3,2,0,1:T(8,128)(2,1)S(1)} all-gather(bf16[2,6,12,896]{3,2,0,1:T(8,128)(2,1)S(1)} %copy.99), channel_id=1, replica_groups=mesh['seq'=32,'mp_0'=4,'mp_1'=2] {'mp_0'}, dimensions={0}, use_global_device_ids=true | all-gather | bytes 1290240 | tf_op jit(solution)/shard_map/all_gather | solution.py:26
  96.3 2.0 maximum_bitcast_fusion
  98.3 4.6 %reshape.204 = bf16[12,96,896]{2,1,0:T(8,128)(2,1)} reshape(bf16[12,8,12,896]{3,2,1,0:T(8,128)(2,1)} %maximum_bitcast_fusion) | data formatting | bytes 4128768 | tf_op jit(solution)/shard_map/reshape | solution.py:36
  103.0 3.2 %convolution_convert_fusion = bf16[12,96,512]{2,1,0:T(8,128)(2,1)S(1)} fusion(bf16[12,96,896]{2,1,0:T(8,128)(2,1)} %reshape.204, bf16[896,256]{1,0:T(8,128)(2,1)} %param.23, bf16[896,256]{1,0:T(8,128)(2,1)} %param.22), kind=kOutput, calls=%fused_computation.36 | convolution fusion | flops 1059389440 | bytes 4161536 | tf_op jit(solution)/shard_map/nle,ef->nlf/dot_general | solution.py:160
  106.1 1.2 fusion.133
  107.3 2.5 %reshape.207 = bf16[6,192,2,128]{3,2,1,0:T(2,128)(2,1)} reshape(bf16[12,96,256]{2,1,0:T(8,128)(2,1)} %get-tuple-element.6) | data formatting | bytes 1179648 | tf_op jit(solution)/shard_map/reshape | solution.py:173
  109.8 2.6 %fusion.87 = f32[6,2,64,192]{3,2,1,0:T(8,128)} fusion(bf16[6,192,2,128]{3,2,1,0:T(2,128)(2,1)} %reshape.207, bf16[6,64,2,128]{3,2,1,0:T(2,128)(2,1)} %reshape.206), kind=kOutput, calls=%fused_computation.92 | convolution fusion | flops 38044608 | bytes 1376256 | tf_op jit(solution)/shard_map/div | solution.py:181
  112.5 2.6 %fusion.32 = f32[6,2,64,192]{3,2,1,0:T(8,128)} fusion(bf16[6,192,2,128]{3,2,1,0:T(2,128)(2,1)} %reshape.207, bf16[6,64,2,128]{3,2,1,0:T(2,128)(2,1)} %reshape.206), kind=kOutput, calls=%fused_computation.44 | convolution fusion | flops 37896192 | bytes 1376256 | tf_op jit(solution)/shard_map/cqhd,ckhd->chqk/dot_general | solution.py:177
  115.0 2.5 %reshape.205 = bf16[6,192,2,128]{3,2,1,0:T(2,128)(2,1)} reshape(bf16[12,96,256]{2,1,0:T(8,128)(2,1)} %get-tuple-element.5) | data formatting | bytes 1179648 | tf_op jit(solution)/shard_map/reshape | solution.py:174
  117.5 2.6 %fusion.53 = bf16[6,64,2,128]{3,1,2,0:T(8,128)(2,1)} fusion(bf16[6,192,2,128]{3,2,1,0:T(2,128)(2,1)} %reshape.205, f32[6,2,64,192]{3,2,1,0:T(8,128)} %fusion.32), kind=kOutput, calls=%fused_computation.57 | convolution fusion | flops 38142912 | bytes 1376256 | tf_op jit(solution)/shard_map/chqk,ckhd->cqhd/dot_general | solution.py:184
  120.1 2.6 %fusion.78 = f32[6,2,64,192]{3,2,1,0:T(8,128)} fusion(bf16[6,192,2,128]{3,2,1,0:T(2,128)(2,1)} %reshape.205, bf16[6,64,2,128]{3,2,1,0:T(2,128)(2,1)} %reshape.209), kind=kOutput, calls=%fused_computation.83 | convolution fusion | flops 37748736 | bytes 1376256 | tf_op jit(solution)/shard_map/cqhd,ckhd->chqk/dot_general | solution.py:196
  122.7 3.2 %fusion.54 = bf16[6,64,2,128]{3,1,2,0:T(8,128)(2,1)} fusion(f32[6,2,64,192]{3,2,1,0:T(8,128)} %fusion.87, f32[6,2,64,192]{3,2,1,0:T(8,128)} %fusion.78, bf16[6,192,2,128]{3,2,1,0:T(2,128)(2,1)} %reshape.207), kind=kOutput, calls=%fused_computation.58 | convolution fusion | flops 38585280 | bytes 1966080 | tf_op jit(solution)/shard_map/chqk,ckhd->cqhd/dot_general | solution.py:206
  125.9 1.3 copy.107
  127.2 1.1 copy.103
  128.3 1.8 select_convert_fusion
  131.6 2.1 pad_maximum_fusion
  133.7 3.3 %fusion.42 = bf16[6,192,2,128]{3,1,2,0:T(8,128)(2,1)} fusion(f32[6,2,64,192]{3,2,1,0:T(8,128)} %fusion.87, f32[6,2,64,192]{3,2,1,0:T(8,128)} %fusion.78, bf16[6,64,2,128]{3,2,1,0:T(2,128)(2,1)} %reshape.206), kind=kOutput, calls=%fused_computation.50 | convolution fusion | flops 38781888 | bytes 1966080 | tf_op jit(solution)/shard_map/chqk,cqhd->ckhd/dot_general | solution.py:210
  137.0 2.5 %copy.109 = bf16[6,192,2,128]{3,2,1,0:T(2,128)(2,1)} copy(bf16[6,192,2,128]{3,1,2,0:T(8,128)(2,1)} %fusion.42) | data formatting | bytes 1179648 | tf_op jit(solution)/shard_map/convert_element_type | solution.py:212
  139.5 2.8 %reshape.211 = bf16[12,96,256]{2,1,0:T(8,128)(2,1)} reshape(bf16[6,192,2,128]{3,2,1,0:T(2,128)(2,1)} %copy.109) | data formatting | bytes 1179648 | tf_op jit(solution)/shard_map/reshape | solution.py:213
  142.3 2.8 %fusion.43 = bf16[6,192,2,128]{3,1,2,0:T(8,128)(2,1)} fusion(bf16[6,64,2,128]{3,2,1,0:T(2,128)(2,1)} %reshape.209, f32[6,2,64,192]{3,2,1,0:T(8,128)} %fusion.32), kind=kOutput, calls=%fused_computation.51 | convolution fusion | flops 38339520 | bytes 1376256 | tf_op jit(solution)/shard_map/chqk,cqhd->ckhd/dot_general | solution.py:202
  145.1 2.5 %copy.111 = bf16[6,192,2,128]{3,2,1,0:T(2,128)(2,1)} copy(bf16[6,192,2,128]{3,1,2,0:T(8,128)(2,1)} %fusion.43) | data formatting | bytes 1179648 | tf_op jit(solution)/shard_map/convert_element_type | solution.py:204
  147.6 2.8 %reshape.212 = bf16[12,96,256]{2,1,0:T(8,128)(2,1)} reshape(bf16[6,192,2,128]{3,2,1,0:T(2,128)(2,1)} %copy.111) | data formatting | bytes 1179648 | tf_op jit(solution)/shard_map/reshape | solution.py:214
  150.3 2.1 fusion.84
  152.5 2.1 add_convert_fusion
  154.6 4.6 %reshape.213 = bf16[12,8,12,896]{3,2,1,0:T(8,128)(2,1)} reshape(bf16[12,96,896]{2,1,0:T(8,128)(2,1)} %add_convert_fusion) | data formatting | bytes 4128768 | tf_op jit(solution)/shard_map/reshape | solution.py:51
  159.2 2.0 copy.112
  161.2 38.6 %all_to_all.15 = bf16[8,12,12,896]{3,2,1,0:T(8,128)(2,1)S(1)} all-to-all(bf16[8,12,12,896]{3,2,1,0:T(8,128)(2,1)S(1)} %copy.112), channel_id=1, replica_groups=mesh['seq'=32,'mp_0'=4,'mp_1'=2] {'mp_0','mp_1'}, dimensions={0} | all-to-all | bytes 4128768 | tf_op jit(solution)/shard_map/all_to_all | solution.py:57
  199.8 1.3 convert_reduce_fusion
  201.2 6.1 %fusion.68 = (f32[12,12]{1,0:T(8,128)}, f32[12,12,896]{2,1,0:T(8,128)}) fusion(f32[12,12]{1,0:T(8,128)} %copy-done.6, bf16[12,12,896]{2,1,0:T(8,128)(2,1)S(1)} %gather_fusion.1, pred[12]{0:T(512)(128)(4,1)} %compare_and_fusion.1, f32[896]{0:T(1024)} %param.18, bf16[896,1792]{1,0:T(8,128)(2,1)S(1)} %copy-done, bf16[1792,896]{1,0:T(8,128)(2,1)} %param.20, ...), kind=kOutput, calls=%fused_computation.73 | convolution fusion | flops 928069504 | bytes 8749708 | tf_op jit(solution)/shard_map/nlf,ef->nle/dot_general | solution.py:102
  207.9 1.5 fusion.71
  210.6 27.8 %all_to_all.16 = bf16[32,12,896]{2,1,0:T(8,128)(2,1)S(1)} all-to-all(bf16[32,12,896]{2,1,0:T(8,128)(2,1)S(1)} %copy.114), channel_id=1, replica_groups=mesh['seq'=32,'mp_0'=4,'mp_1'=2] {'seq'}, dimensions={0} | all-to-all | bytes 1376256 | tf_op jit(solution)/shard_map/all_to_all | solution.py:228
  238.4 1.0 fusion.73
  239.4 1.9 slice_convert_fusion
  (78 shorter events, 11.7 us)
Async XLA Ops:
  7.2 47.3 %copy-start = (bf16[896,1792]{1,0:T(8,128)(2,1)S(1)}, bf16[896,1792]{1,0:T(8,128)(2,1)}, u32[]{:S(2)}) copy-start(bf16[896,1792]{1,0:T(8,128)(2,1)} %param.19) | copy-start | bytes 9633796
  11.1 0.6 copy-start.15
  16.6 14.3 %copy-start.9 = (f32[2048]{0:T(1024)S(1)}, f32[2048]{0:T(1024)}, u32[]{:S(2)}) copy-start(f32[2048]{0:T(1024)} %param.17) | copy-start | bytes 24580
  16.6 34.4 %all-to-all-start = ((bf16[32,12,896]{2,1,0:T(8,128)(2,1)}), bf16[32,12,896]{2,1,0:T(8,128)(2,1)}, u32[]{:S(2)}, u32[]{:S(2)}) async-start(bf16[32,12,896]{2,1,0:T(8,128)(2,1)} %broadcast_select_fusion), calls=%async_computation | async-start | bytes 1835008 | tf_op jit(solution)/shard_map/all_to_all | solution.py:157
  28.9 210.5 %reduce-scatter.2.cloned.1.call-start = ((), (), s32[]{:S(2)}) async-start(), calls=%async_computation.4 | async-start | bytes 3538944 | tf_op jit(solution)/shard_map/reduce_scatter | solution.py:63
  29.1 4.9 %copy-start.18 = (pred[384]{0:T(512)(128)(4,1)}, pred[384]{0:T(512)(128)(4,1)S(1)}, u32[]{:S(2)}) copy-start(pred[384]{0:T(512)(128)(4,1)S(1)} %broadcast_in_dim.71) | copy-start | bytes 1156
  30.9 2.3 copy-start.7
  37.3 0.6 copy-start.12
  53.9 0.6 copy-start.6
  54.5 1.8 copy-start.11
  54.5 1.9 copy-start.17
  56.4 1.2 copy-start.3
  125.9 4.3 %copy-start.1 = (bf16[384,2048]{1,0:T(8,128)(2,1)S(1)}, bf16[384,2048]{1,0:T(8,128)(2,1)}, u32[]{:S(2)}) copy-start(bf16[384,2048]{1,0:T(8,128)(2,1)} %param.13) | copy-start | bytes 4718596
  125.9 4.3 %copy-start.4 = (bf16[2048,256]{1,0:T(8,128)(2,1)S(1)}, bf16[2048,256]{1,0:T(8,128)(2,1)}, u32[]{:S(2)}) copy-start(bf16[2048,256]{1,0:T(8,128)(2,1)} %param.21) | copy-start | bytes 3145732
  125.9 4.3 %copy-start.8 = (f32[384]{0:T(512)S(1)}, f32[384]{0:T(512)}, u32[]{:S(2)}) copy-start(f32[384]{0:T(512)} %copy-done.7) | copy-start | bytes 4612
  125.9 4.3 %copy-start.10 = (f32[2048]{0:T(1024)S(1)}, f32[2048]{0:T(1024)}, u32[]{:S(2)}) copy-start(f32[2048]{0:T(1024)} %param.17) | copy-start | bytes 24580
  150.3 2.1 copy-start.2
  150.3 2.1 copy-start.5
  207.2 2.2 copy-start.13
  210.3 28.1 %copy-start.14 = (pred[32]{0:T(512)(128)(4,1)S(1)}, pred[32]{0:T(512)(128)(4,1)}, u32[]{:S(2)}) copy-start(pred[32]{0:T(512)(128)(4,1)} %get-tuple-element.3) | copy-start | bytes 100
  210.3 28.1 %copy-start.16 = (s32[32]{0:T(128)S(1)}, s32[32]{0:T(128)}, u32[]{:S(2)}) copy-start(s32[32]{0:T(128)} %copy-done.15) | copy-start | bytes 388
Sparse Core Ops, SparseCore 0:
  133.8 32.7 reduce-scatter.1
where the time goes:
time: 252 us; the launch traced here: 248 us
  blocking collectives  105 us (42%)
  matrix products  44.9 us (18%)
  local copies, waits for them, and re-layouts  41 us (16%)
  other arithmetic  17.9 us (7%)
  between operations  14.4 us (6%)
  waiting for transfers between devices  12.6 us (5%)
  starting transfers between devices  12.3 us (5%)
    all_to_all x1, blocking collectives, summed_on_arrival(): tiles = lax.all_to_all(split_up(x, dim, devices), axis, 0, 0, tiled=True)  38.6 us
    all_gather x4, blocking collectives, gather_in_order(): tiles = lax.all_gather(tiles, axes[k], axis=0, tiled=True)  38.5 us
    all_to_all x1, blocking collectives, body(): lax.all_to_all(returned.astype(jnp.bfloat16), 'seq', split_axis=0, concat...  27.8 us
    all_to_all x1, waiting for transfers between devices, body(): lax.all_to_all(outgoing, 'seq', split_axis=0, concat_axis=0, tiled=True)  12.6 us
    all_to_all x1, starting transfers between devices, body(): lax.all_to_all(outgoing, 'seq', split_axis=0, concat_axis=0, tiled=True)  12.3 us
    dot_general x1, matrix products, encode_back(): jnp.einsum('nlf,ef->nle', grad_pre, w_in, preferred_element_type=jnp.floa...  6.08 us
  transfers between devices with their start and end apart: 2, of which 1 were waited for; matrix products, arithmetic and copies ran while one was open for 20% of the time, Pallas kernels for 0%

commit v1 on v0

v1 whole, which is shorter than its diff:
```python
import functools

import jax
import jax.numpy as jnp
from jax import lax
from jax.experimental import pallas as pl
from jax.experimental.pallas import tpu as pltpu
from jax.sharding import Mesh
from jax.sharding import PartitionSpec as P

HD = 128
STRETCH = 64
K = 2
SEQ_LEN = 4096
UNIT = 8
EPSILON = 1e-06
MP = ("mp_0", "mp_1")
F32 = jnp.float32
BF16 = jnp.bfloat16
VM = pl.BlockSpec(memory_space=pltpu.VMEM)
SM = pl.BlockSpec(memory_space=pltpu.SMEM)
HB = pl.BlockSpec(memory_space=pltpu.HBM)
BIG = 64000 * 1024


def rcopy(src, dst, ssem, rsem, **where):
    return pltpu.make_async_remote_copy(
        src_ref=src,
        dst_ref=dst,
        send_sem=ssem,
        recv_sem=rsem,
        device_id=where,
        device_id_type=pl.DeviceIdType.MESH,
    )


def dot(a, b, ca=1, cb=0):
    return lax.dot_general(a, b, (((ca,), (cb,)), ((), ())), preferred_element_type=F32)


def rms_scaling(values):
    return lax.rsqrt(jnp.mean(values * values, axis=-1, keepdims=True) + EPSILON)


def sigmoid(v):
    return 1.0 / (1.0 + jnp.exp(-v))


def greet(n_seq, nx):
    me, x, c = lax.axis_index("seq"), lax.axis_index("mp_0"), lax.axis_index("mp_1")
    barrier = pltpu.get_barrier_semaphore()

    def tell(**where):
        pl.semaphore_signal(barrier, inc=1, device_id=where, device_id_type=pl.DeviceIdType.MESH)

    def far(k, carry):
        tell(seq=lax.rem(me + k, n_seq))
        return carry

    lax.fori_loop(1, n_seq, far, 0)
    tell(mp_0=lax.rem(x + 1, nx))
    tell(mp_0=lax.rem(x + nx - 1, nx))
    tell(mp_1=1 - c)
    return barrier, n_seq + 2


def seq_exchange(n_seq, n, src, dst, send, recv):
    me = lax.axis_index("seq")

    def piece(k, sending):
        peer = lax.rem(me + k, n_seq) if sending else lax.rem(me + n_seq - k, n_seq)
        at = me if sending else peer
        return rcopy(
            src.at[peer, pl.ds(0, n)],
            dst.at[at, pl.ds(0, n)],
            send.at[peer],
            recv.at[at],
            seq=peer,
        )

    def start():
        def go(k, carry):
            piece(k, True).start()
            return carry

        lax.fori_loop(1, n_seq, go, 0)

    def arrive():
        def go(k, carry):
            piece(k, False).wait_recv()
            return carry

        lax.fori_loop(1, n_seq, go, 0)

    def drain():
        def go(k, carry):
            piece(k, True).wait_send()
            return carry

        lax.fori_loop(1, n_seq, go, 0)

    return start, arrive, drain


def fetch_kernel(
    dims,
    codes, db, egain, w_in, w_out, tok, gout, dgain, w_q, w_p,
    full, q, gctx,
    win_v, w_in_v, w_out_v, tok_v, gout_v, w_q_v, w_p_v, enc, outg, recv, rows_s,
    lsem, a_send, a_recv, b_send, b_recv,
):
    n_seq, nx, nb, rows_dev, e = dims
    me, x, c = lax.axis_index("seq"), lax.axis_index("mp_0"), lax.axis_index("mp_1")
    barrier, greeted = greet(n_seq, nx)
    loads = [
        pltpu.make_async_copy(s, d, lsem.at[i])
        for i, (s, d) in enumerate(
            (
                (db.at[:, pl.ds(3 * x + c, 2)], win_v),
                (w_in, w_in_v),
                (w_out, w_out_v),
                (tok, tok_v),
                (w_q, w_q_v),
                (gout, gout_v),
                (w_p, w_p_v),
            )
        )
    ]
    for load in loads:
        load.start()

    def find(d, carry):
        row = jnp.int32(0)
        for k in range(nb):
            code = codes[d * nb + k]
            row = jnp.where(code // rows_dev == me, lax.rem(code, rows_dev), row)
        rows_s[d] = row
        return carry

    lax.fori_loop(0, n_seq, find, 0)

    loads[0].wait()
    values = win_v[...].astype(F32).reshape(rows_dev * 2 * UNIT, e)
    normed = (values * rms_scaling(values) * egain[...]).astype(BF16)
    loads[1].wait()
    pre = dot(normed, w_in_v[...])
    hidden = (pre * sigmoid(pre)).astype(BF16)
    loads[2].wait()
    encoded = values + dot(hidden, w_out_v[...])
    enc[...] = encoded.reshape(rows_dev, 2, UNIT, e).astype(BF16)

    def stage(d, carry):
        outg[d] = enc[rows_s[d]]
        return carry

    lax.fori_loop(0, n_seq, stage, 0)
    recv[me] = outg[me]
    pl.semaphore_wait(barrier, greeted)

    plans = {n: seq_exchange(n_seq, n, outg, recv, a_send, a_recv) for n in (1, 2)}
    for n in (1, 2):
        @pl.when(c == n - 1)
        def _(n=n):
            plans[n][0]()

    size = min(128, q.shape[0])
    blocks = q.shape[0] // size
    loads[3].wait()
    loads[4].wait()

    def query(i, carry):
        at = pl.ds(pl.multiple_of(i * size, size), size)
        vals = tok_v[at, :].astype(F32)
        unit = (vals * rms_scaling(vals) * dgain[...]).astype(BF16)
        q[at, :] = dot(unit, w_q_v[...]).astype(BF16)
        return carry

    lax.fori_loop(0, blocks, query, 0)
    loads[5].wait()
    loads[6].wait()

    def context_grad(i, carry):
        at = pl.ds(pl.multiple_of(i * size, size), size)
        where = me * q.shape[0] + i * size + lax.broadcasted_iota(jnp.int32, (size, 1), 0)
        live = lax.rem(where // STRETCH, SEQ_LEN // STRETCH) != 0
        grad = dot(gout_v[at, :], w_p_v[...], 1, 1)
        gctx[at, :] = jnp.where(live, grad, 0.0).astype(BF16)
        return carry

    lax.fori_loop(0, blocks, context_grad, 0)

    half = nb // 2
    right, left, opp = lax.rem(x + 1, nx), lax.rem(x + nx - 1, nx), lax.rem(x + 2, nx)
    for n in (1, 2):
        @pl.when(c == n - 1)
        def _(n=n):
            plans[n][1]()
            other = 3 - n

            def mine(xx, n=n):
                return full.at[:, pl.ds(3 * xx + n - 1, n)]

            def part(xx, h, n=n):
                return full.at[pl.ds(half * h, half), pl.ds(3 * xx + n - 1, n)]

            def pick(j, carry):
                slot = codes[me * nb + j] // rows_dev
                for i in range(n):
                    full[j, 3 * x + n - 1 + i] = recv[slot, i]
                return carry

            lax.fori_loop(0, nb, pick, 0)
            moved = []

            def send(i, ref, **where):
                copy = rcopy(ref, ref, b_send.at[i], b_recv.at[i], **where)
                copy.start()
                moved.append(copy)

            def got(i, ref, **where):
                rcopy(ref, ref, b_send.at[i], b_recv.at[i], **where).wait_recv()

            send(0, mine(x), mp_0=right)
            send(1, mine(x), mp_0=left)
            send(2, mine(x), mp_1=1 - c)
            got(0, mine(left), mp_0=left)
            send(3, part(left, 0), mp_0=right)
            send(4, mine(left), mp_1=1 - c)
            got(1, mine(right), mp_0=right)
            send(5, part(right, 1), mp_0=left)
            send(6, mine(right), mp_1=1 - c)
            got(3, part(opp, 0), mp_0=left)
            send(7, part(opp, 0), mp_1=1 - c)
            got(5, part(opp, 1), mp_0=right)
            send(8, part(opp, 1), mp_1=1 - c)
            got(2, mine(x, other), mp_1=1 - c)
            got(4, mine(left, other), mp_1=1 - c)
            got(6, mine(right, other), mp_1=1 - c)
            got(7, part(opp, 0, other), mp_1=1 - c)
            got(8, part(opp, 1, other), mp_1=1 - c)
            for copy in moved:
                copy.wait_send()
            plans[n][2]()


def fetch(dims, codes, db, egain, w_in, w_out, tok, gout, dgain, w_q, w_p):
    n_seq, nx, nb, rows_dev, e = dims
    slot = (2, UNIT, e)
    return pl.pallas_call(
        functools.partial(fetch_kernel, dims),
        out_shape=(
            jax.ShapeDtypeStruct((nb, db.shape[1], UNIT, e), BF16),
            jax.ShapeDtypeStruct((tok.shape[0], w_q.shape[1]), BF16),
            jax.ShapeDtypeStruct((tok.shape[0], w_q.shape[1]), BF16),
        ),
        in_specs=[SM, HB, VM, HB, HB, HB, HB, VM, HB, HB],
        out_specs=(VM, VM, VM),
        scratch_shapes=[
            pltpu.VMEM((rows_dev, *slot), BF16),
            pltpu.VMEM(w_in.shape, BF16),
            pltpu.VMEM(w_out.shape, BF16),
            pltpu.VMEM(tok.shape, BF16),
            pltpu.VMEM(gout.shape, BF16),
            pltpu.VMEM(w_q.shape, BF16),
            pltpu.VMEM(w_p.shape, BF16),
            pltpu.VMEM((rows_dev, *slot), BF16),
            pltpu.VMEM((n_seq, *slot), BF16),
            pltpu.VMEM((n_seq, *slot), BF16),
            pltpu.SMEM((n_seq,), jnp.int32),
            pltpu.SemaphoreType.DMA((7,)),
            pltpu.SemaphoreType.DMA((n_seq,)),
            pltpu.SemaphoreType.DMA((n_seq,)),
            pltpu.SemaphoreType.DMA((9,)),
            pltpu.SemaphoreType.DMA((9,)),
        ],
        compiler_params=pltpu.CompilerParams(
            collective_id=0, has_side_effects=True, vmem_limit_bytes=BIG
        ),
        name="fetch",
    )(codes, db, egain, w_in, w_out, tok, gout, dgain, w_q, w_p)


def attend_kernel(per, full, q, gctx, w_k, w_v, terms, ctx, dq):
    heads = q.shape[1] // HD
    span = full.shape[0] // per
    factor = HD ** (-0.5)
    keys, vals = [], []
    for s in range(per):
        rows = full[s * span:(s + 1) * span, :]
        keys.append(dot(rows, w_k[...]).astype(BF16))
        vals.append(dot(rows, w_v[...]).astype(BF16))
    todo = [(s, h) for s in range(per) for h in range(heads)]
    at = {
        (s, h): (slice(s * STRETCH, (s + 1) * STRETCH), slice(h * HD, (h + 1) * HD))
        for s, h in todo
    }
    qs = {t: q[at[t]] for t in todo}
    gs = {t: gctx[at[t]] for t in todo}
    ks = {(s, h): keys[s][:, h * HD:(h + 1) * HD] for s, h in todo}
    vs = {(s, h): vals[s][:, h * HD:(h + 1) * HD] for s, h in todo}
    exps = {t: jnp.exp(dot(qs[t], ks[t], 1, 1) * factor) for t in todo}
    dps = {t: dot(gs[t], vs[t], 1, 1) for t in todo}
    probs = {t: exps[t] / jnp.sum(exps[t], axis=-1, keepdims=True) for t in todo}
    weights = {t: probs[t].astype(BF16) for t in todo}
    scores = {
        t: (
            probs[t] * (dps[t] - jnp.sum(probs[t] * dps[t], axis=-1, keepdims=True)) * factor
        ).astype(BF16)
        for t in todo
    }
    for t in todo:
        ctx[at[t]] = dot(weights[t], vs[t]).astype(BF16)
        dq[at[t]] = dot(scores[t], ks[t]).astype(BF16)
    dks = {t: dot(scores[t], qs[t], 0, 0).astype(BF16) for t in todo}
    dvs = {t: dot(weights[t], gs[t], 0, 0).astype(BF16) for t in todo}
    for s in range(per):
        dk = jnp.concatenate([dks[(s, h)] for h in range(heads)], axis=1)
        dv = jnp.concatenate([dvs[(s, h)] for h in range(heads)], axis=1)
        out = dot(dk, w_k[...], 1, 1) + dot(dv, w_v[...], 1, 1)
        terms[s * span:(s + 1) * span, :] = out.astype(BF16)


def attend(full, q, gctx, w_k, w_v, per):
    steps = q.shape[0] // STRETCH // per
    rows, e = full.shape
    width = q.shape[1]

    def cut(r, w):
        return pl.BlockSpec((r // steps, w), lambda i: (i, 0))

    def whole(a):
        return pl.BlockSpec(a.shape, lambda i: (0, 0))

    return pl.pallas_call(
        functools.partial(attend_kernel, per),
        grid=(steps,),
        out_shape=(
            jax.ShapeDtypeStruct(full.shape, BF16),
            jax.ShapeDtypeStruct(q.shape, BF16),
            jax.ShapeDtypeStruct(q.shape, BF16),
        ),
        in_specs=[cut(rows, e), cut(q.shape[0], width), cut(q.shape[0], width), whole(w_k), whole(w_v)],
        out_specs=(cut(rows, e), cut(q.shape[0], width), cut(q.shape[0], width)),
        compiler_params=pltpu.CompilerParams(vmem_limit_bytes=BIG),
        name="attend",
    )(full, q, gctx, w_k, w_v)


def return_kernel(
    dims,
    codes, terms, ctx, dq, tok, dgain, w_q, w_p,
    recv, own, fin,
    sib, relay, last, comb, ge, back, gn, outs, osib, orelay, ocomb, pick_s,
    d_send, d_recv, o_send, o_recv, e_send, e_recv, f_send, f_recv,
):
    n_seq, nx, nb, rows_dev, e = dims
    me, x, c = lax.axis_index("seq"), lax.axis_index("mp_0"), lax.axis_index("mp_1")
    barrier, greeted = greet(n_seq, nx)
    half = nb // 2
    right, left, opp = lax.rem(x + 1, nx), lax.rem(x + nx - 1, nx), lax.rem(x + 2, nx)
    branches = (1, 2)

    def each(f):
        for n in branches:
            @pl.when(c == n - 1)
            def _(n=n):
                f(n)

    def pairs(n):
        other = 3 - n
        return [
            (
                rcopy(
                    terms.at[:, pl.ds(3 * k + other - 1, other)],
                    sib.at[k, :, pl.ds(0, other)],
                    d_send.at[k],
                    d_recv.at[k],
                    mp_1=1 - c,
                ),
                rcopy(
                    terms.at[:, pl.ds(3 * k + n - 1, n)],
                    sib.at[k, :, pl.ds(0, n)],
                    d_send.at[k],
                    d_recv.at[k],
                    mp_1=1 - c,
                ),
            )
            for k in range(nx)
        ]

    def find(s, carry):
        spot = jnp.int32(0)
        for k in range(nb):
            spot = jnp.where(codes[me * nb + k] // rows_dev == s, k, spot)
        pick_s[s] = spot
        return carry

    lax.fori_loop(0, n_seq, find, 0)
    pl.semaphore_wait(barrier, greeted)

    def pair_start(n):
        for sent, _ in pairs(n):
            sent.start()

    each(pair_start)

    rows = ctx.shape[0]
    lanes = 2 * nx
    cols = tok.shape[2]
    live = lax.rem(
        (me * rows + lax.broadcasted_iota(jnp.int32, (rows, 1), 0)) // STRETCH, SEQ_LEN // STRETCH
    ) != 0

    def squares(l, total):
        vals = tok[l].astype(F32)
        return total + jnp.sum(vals * vals, axis=-1, keepdims=True)

    scaling = lax.rsqrt(
        lax.fori_loop(0, lanes, squares, jnp.zeros((rows, 1), F32)) / (lanes * cols) + EPSILON
    )

    def forward(l, total):
        out = dot(ctx[...], w_p[l])
        outs[l // 2, lax.rem(l, 2), 0] = jnp.where(live, out, 0.0).astype(BF16)
        grad = dot(dq[...], w_q[l], 1, 1) * dgain[l]
        gn[l] = grad
        return total + jnp.sum(grad * tok[l].astype(F32), axis=-1, keepdims=True)

    total = lax.fori_loop(0, lanes, forward, jnp.zeros((rows, 1), F32))
    slope = total * scaling * scaling / (lanes * cols)

    def finish(l, carry):
        grad = scaling * (gn[l] - tok[l].astype(F32) * slope)
        outs[l // 2, lax.rem(l, 2), 1] = grad.astype(BF16)
        return carry

    lax.fori_loop(0, lanes, finish, 0)

    def reduce_first(n):
        for (_, got), k in zip(pairs(n), range(nx)):
            got.wait_recv()

        def add(i, carry):
            k, j = i // nb, lax.rem(i, nb)
            for u in range(n):
                comb[k, j, u] = (
                    terms[j, 3 * k + n - 1 + u].astype(F32) + sib[k, j, u].astype(F32)
                ).astype(BF16)
            return carry

        lax.fori_loop(0, nx * nb, add, 0)

    each(reduce_first)

    def relays(n):
        return [
            rcopy(
                comb.at[opp, pl.ds(half * h, half), pl.ds(0, n)],
                relay.at[h, :, pl.ds(0, n)],
                d_send.at[nx + h],
                d_recv.at[nx + h],
                mp_0=to,
            )
            for h, to in ((0, right), (1, left))
        ]

    def ends(n):
        return [
            rcopy(
                comb.at[to, :, pl.ds(0, n)],
                last.at[h, :, pl.ds(0, n)],
                d_send.at[nx + 2 + h],
                d_recv.at[nx + 2 + h],
                mp_0=to,
            )
            for h, to in ((0, right), (1, left))
        ]

    def relay_start(n):
        for copy in relays(n):
            copy.start()

    each(relay_start)

    def out_pair():
        return [
            rcopy(outs.at[k, 1 - c], osib.at[k], o_send.at[k], o_recv.at[k], mp_1=1 - c)
            for k in range(nx)
        ]

    for copy in out_pair():
        copy.start()

    def relay_end(n):
        for h, copy in enumerate(relays(n)):
            copy.wait_recv()

        for h, to in ((0, right), (1, left)):

            def add(j, carry, h=h, to=to):
                for u in range(n):
                    comb[to, half * h + j, u] = (
                        comb[to, half * h + j, u].astype(F32) + relay[h, j, u].astype(F32)
                    ).astype(BF16)
                return carry

            lax.fori_loop(0, half, add, 0)
        for copy in ends(n):
            copy.start()

    each(relay_end)

    for k, copy in enumerate(out_pair()):
        copy.wait_recv()

        def add(i, carry, k=k):
            at = pl.ds(pl.multiple_of(i * STRETCH, STRETCH), STRETCH)
            for t in range(2):
                ocomb[k, t, at, :] = (
                    outs[k, c, t, at, :].astype(F32) + osib[k, t, at, :].astype(F32)
                ).astype(BF16)
            return carry

        lax.fori_loop(0, rows // STRETCH, add, 0)
    own[...] = ocomb[x]

    def out_relays():
        return [
            rcopy(ocomb.at[opp, h], orelay.at[h], o_send.at[nx + h], o_recv.at[nx + h], mp_0=to)
            for h, to in ((0, right), (1, left))
        ]

    def out_ends():
        return [
            rcopy(ocomb.at[to], fin.at[h], o_send.at[nx + 2 + h], o_recv.at[nx + 2 + h], mp_0=to)
            for h, to in ((0, right), (1, left))
        ]

    for copy in out_relays():
        copy.start()

    plans = {n: seq_exchange(n_seq, n, back, recv, e_send, e_recv) for n in branches}

    def give_back(n):
        for copy in ends(n):
            copy.wait_recv()

        def add(j, carry):
            for u in range(n):
                ge[j, u] = (
                    comb[x, j, u].astype(F32)
                    + last[0, j, u].astype(F32)
                    + last[1, j, u].astype(F32)
                ).astype(BF16)
            return carry

        lax.fori_loop(0, nb, add, 0)

        def stage(s, carry):
            spot = pick_s[s]
            for u in range(n):
                back[s, u] = ge[spot, u]
            return carry

        lax.fori_loop(0, n_seq, stage, 0)
        for u in range(n):
            recv[me, u] = back[me, u]
        plans[n][0]()

    each(give_back)

    for h, (copy, to) in enumerate(zip(out_relays(), (right, left))):
        copy.wait_recv()

        def add(i, carry, h=h, to=to):
            at = pl.ds(pl.multiple_of(i * STRETCH, STRETCH), STRETCH)
            ocomb[to, h, at, :] = (
                ocomb[to, h, at, :].astype(F32) + orelay[h, at, :].astype(F32)
            ).astype(BF16)
            return carry

        lax.fori_loop(0, rows // STRETCH, add, 0)
    for copy in out_ends():
        copy.start()

    shared = rcopy(recv.at[:, 0], recv.at[:, 1], f_send, f_recv, mp_1=1 - c)

    def settle(n):
        plans[n][1]()
        if n == 2:
            shared.start()
        else:
            shared.wait_recv()
        plans[n][2]()
        for sent, _ in pairs(n):
            sent.wait_send()
        for copy in relays(n) + ends(n):
            copy.wait_send()
        if n == 2:
            shared.wait_send()

    each(settle)
    for copy in out_ends():
        copy.wait_recv()
    for copy in out_pair() + out_relays() + out_ends():
        copy.wait_send()


def give(dims, codes, terms, ctx, dq, tok, dgain, w_q, w_p):
    n_seq, nx, nb, rows_dev, e = dims
    rows = ctx.shape[0]
    lanes, _, cols = tok.shape
    half = nb // 2
    slot = (2, UNIT, e)
    return pl.pallas_call(
        functools.partial(return_kernel, dims),
        out_shape=(
            jax.ShapeDtypeStruct((n_seq, *slot), BF16),
            jax.ShapeDtypeStruct((2, rows, cols), BF16),
            jax.ShapeDtypeStruct((2, 2, rows, cols), BF16),
        ),
        in_specs=[SM] + [VM] * 7,
        out_specs=(VM, VM, VM),
        scratch_shapes=[
            pltpu.VMEM((nx, nb, *slot), BF16),
            pltpu.VMEM((2, half, *slot), BF16),
            pltpu.VMEM((2, nb, *slot), BF16),
            pltpu.VMEM((nx, nb, *slot), BF16),
            pltpu.VMEM((nb, *slot), BF16),
            pltpu.VMEM((n_seq, *slot), BF16),
            pltpu.VMEM((lanes, rows, cols), F32),
            pltpu.VMEM((nx, 2, 2, rows, cols), BF16),
            pltpu.VMEM((nx, 2, rows, cols), BF16),
            pltpu.VMEM((2, rows, cols), BF16),
            pltpu.VMEM((nx, 2, rows, cols), BF16),
            pltpu.SMEM((n_seq,), jnp.int32),
            pltpu.SemaphoreType.DMA((nx + 4,)),
            pltpu.SemaphoreType.DMA((nx + 4,)),
            pltpu.SemaphoreType.DMA((nx + 4,)),
            pltpu.SemaphoreType.DMA((nx + 4,)),
            pltpu.SemaphoreType.DMA((n_seq,)),
            pltpu.SemaphoreType.DMA((n_seq,)),
            pltpu.SemaphoreType.DMA,
            pltpu.SemaphoreType.DMA,
        ],
        compiler_params=pltpu.CompilerParams(
            collective_id=1, has_side_effects=True, vmem_limit_bytes=BIG
        ),
        name="give",
    )(codes, terms, ctx, dq, tok, dgain, w_q, w_p)


def settle_kernel(dims, codes, recv, own, fin, db, egain, w_in, w_out, cca, gtok, gdb, win_v, acc, lsem):
    n_seq, nx, nb, rows_dev, e = dims
    me, x, c = lax.axis_index("seq"), lax.axis_index("mp_0"), lax.axis_index("mp_1")
    load = pltpu.make_async_copy(db.at[:, pl.ds(3 * x + c, 2)], win_v, lsem)
    load.start()
    cca[...] = (own[0].astype(F32) + fin[0, 0].astype(F32) + fin[1, 0].astype(F32)).astype(BF16)
    gtok[...] = own[1].astype(F32) + fin[0, 1].astype(F32) + fin[1, 1].astype(F32)
    acc[...] = jnp.zeros_like(acc)

    def gather(d, carry):
        for k in range(nb):
            code = codes[d * nb + k]

            @pl.when(code // rows_dev == me)
            def _():
                r = lax.rem(code, rows_dev)
                acc[r] = acc[r] + recv[d].astype(F32)

        return carry

    lax.fori_loop(0, n_seq, gather, 0)
    grad_enc = acc[...].reshape(rows_dev * 2 * UNIT, e)
    load.wait()
    values = win_v[...].astype(F32).reshape(rows_dev * 2 * UNIT, e)
    scaling = rms_scaling(values)
    unit = values * scaling
    pre = dot((unit * egain[...]).astype(BF16), w_in[...])
    s = sigmoid(pre)
    grad_hidden = dot(grad_enc.astype(BF16), w_out[...], 1, 1)
    grad_pre = (grad_hidden * (s * (1.0 + pre * (1.0 - s)))).astype(BF16)
    g = dot(grad_pre, w_in[...], 1, 1) * egain[...]
    out = grad_enc + scaling * (g - unit * jnp.mean(g * unit, axis=-1, keepdims=True))
    out = out.reshape(rows_dev, 2 * UNIT, e)
    keep = gdb.shape[1]
    for n in range(2):
        @pl.when(c == n)
        def _(n=n):
            gdb[...] = out[:, (2 * UNIT - keep) * n:(2 * UNIT - keep) * n + keep, :]


def settle(dims, codes, recv, own, fin, db, egain, w_in, w_out):
    n_seq, nx, nb, rows_dev, e = dims
    return pl.pallas_call(
        functools.partial(settle_kernel, dims),
        out_shape=(
            jax.ShapeDtypeStruct(own.shape[1:], BF16),
            jax.ShapeDtypeStruct(own.shape[1:], F32),
            jax.ShapeDtypeStruct((rows_dev, 3 * UNIT // 2, e), F32),
        ),
        in_specs=[SM, VM, VM, VM, HB, VM, VM, VM],
        out_specs=(VM, VM, VM),
        scratch_shapes=[
            pltpu.VMEM((rows_dev, 2, UNIT, e), BF16),
            pltpu.VMEM((rows_dev, 2, UNIT, e), F32),
            pltpu.SemaphoreType.DMA,
        ],
        compiler_params=pltpu.CompilerParams(vmem_limit_bytes=BIG),
        name="settle",
    )(codes, recv, own, fin, db, egain, w_in, w_out)


def body(
    n_seq, nx,
    tokens, database, nb_shard, nb_row, dec_gain, enc_gain,
    w_in, w_out, w_query, w_key, w_value, w_proj, grad_out,
):
    rows_dev, length, e = database.shape
    rows, d = tokens.shape
    width = w_query.shape[1]
    nb = rows // STRETCH * K
    lanes = 2 * nx
    dims = (n_seq, nx, nb, rows_dev, e)
    codes = (nb_shard * rows_dev + nb_row).reshape(-1)
    db = database.reshape(rows_dev, length // UNIT, UNIT, e)
    egain = enc_gain.reshape(1, e)
    full, q, gctx = fetch(
        dims, codes, db, egain, w_in, w_out, tokens, grad_out, dec_gain.reshape(1, d), w_query, w_proj
    )
    terms, ctx, dq = attend(
        full.reshape(nb * length, e), q, gctx, w_key, w_value, max(1, nb // K // 2)
    )
    tok = tokens.reshape(rows, lanes, d // lanes).transpose(1, 0, 2)
    w_p = w_proj.reshape(width, lanes, d // lanes).transpose(1, 0, 2)
    w_q = w_query.reshape(lanes, d // lanes, width)
    recv, own, fin = give(
        dims, codes, terms.reshape(full.shape), ctx, dq, tok, dec_gain.reshape(lanes, 1, d // lanes), w_q, w_p
    )
    return settle(dims, codes, recv, own, fin, db, egain, w_in, w_out)


def solution(mesh):
    n_seq = mesh.shape["seq"]
    nx = mesh.shape["mp"] // 2
    split = Mesh(mesh.devices.reshape(n_seq, nx, 2), ("seq", "mp_0", "mp_1"))
    placed = (
        P("seq", None),
        P("seq", None, None),
        P(),
        P(),
        P(),
        P(),
        P(),
        P(),
        P(None, MP),
        P(None, MP),
        P(None, MP),
        P(MP, None),
        P("seq", None),
    )
    return jax.shard_map(
        functools.partial(body, n_seq, nx),
        mesh=split,
        in_specs=placed,
        out_specs=(P("seq", MP), P("seq", MP), P("seq", MP, None)),
        check_vma=False,
    )
```

time: 252 us -> 124 us (0.49); the launches traced: 248 us -> 124 us
  Pallas kernels: 0 us -> 113 us
  blocking collectives: 105 us -> 0 us
  matrix products: 44.9 us -> 0 us
  local copies, waits for them, and re-layouts: 41 us -> 9.3 us
  other arithmetic: 17.9 us -> 0.7 us
  between operations: 14.4 us -> 0.69 us
  waiting for transfers between devices: 12.6 us -> 0 us
  starting transfers between devices: 12.3 us -> 0 us
    pallas_call x0 -> x4, Pallas kernels: none -> 113 us  [the longest x1 48.6 us: give(): pl.pallas_call(functools.partial(return_kernel, dims), out_shape=(jax.Sha...]
    all_to_all x2 -> x0, blocking collectives: 66.4 us -> none  [the longest x1 38.6 us: summed_on_arrival(): tiles = lax.all_to_all(split_up(x, dim, devices), axis, 0, 0, tiled=True)]
    dot_general x18 -> x0, matrix products: 42.2 us -> none  [the longest x1 6.08 us: encode_back(): jnp.einsum('nlf,ef->nle', grad_pre, w_in, preferred_element_type=jnp.floa...]
    all_gather x4 -> x0, blocking collectives: 38.5 us -> none  [gather_in_order(): tiles = lax.all_gather(tiles, axes[k], axis=0, tiled=True)]
    reshape x10 -> x4, local copies, waits for them, and re-layouts: 21.4 us -> 4.93 us  [the longest x1 1.62 us: body(): tok = tokens.reshape(rows, lanes, d // lanes).transpose(1, 0, 2)]
    all_to_all x1 -> x0, waiting for transfers between devices: 12.6 us -> none  [body(): lax.all_to_all(outgoing, 'seq', split_axis=0, concat_axis=0, tiled=True)]
    all_to_all x1 -> x0, starting transfers between devices: 12.3 us -> none  [body(): lax.all_to_all(outgoing, 'seq', split_axis=0, concat_axis=0, tiled=True)]
    convert_element_type x5 -> x0, local copies, waits for them, and re-layouts: 7.62 us -> none  [the longest x1 2.5 us: body(): grad_key = jnp.einsum('chqk,cqhd->ckhd', grad_score, query_blk, preferred...]
  transfers between devices with their start and end apart: 2 -> 0, of which waited for: 1 -> 0; matrix products, arithmetic and copies ran while one was open for 20% -> 0% of each run, Pallas kernels for 0% -> 0%
where the time goes in v1:
time: 124 us
  Pallas kernels  113 us (91%)
  local copies, waits for them, and re-layouts  9.3 us (8%)
    pallas_call x1, Pallas kernels, give(): pl.pallas_call(functools.partial(return_kernel, dims), out_shape=(jax.Sha...  48.6 us
    pallas_call x1, Pallas kernels, fetch(): pl.pallas_call(functools.partial(fetch_kernel, dims), out_shape=(jax.Shap...  43.2 us
    pallas_call x1, Pallas kernels, settle(): pl.pallas_call(functools.partial(settle_kernel, dims), out_shape=(jax.Sha...  13.4 us
    pallas_call x1, Pallas kernels, attend(): pl.pallas_call(functools.partial(attend_kernel, per), grid=(steps,), out_...  7.86 us

profile of v1, /device:TPU:1, one launch (start us, length us, event | category | flops | bytes accessed | tf_op | source)
XLA Modules:
  0.0 123.8 jit_solution(3861334345262701)
XLA Ops:
  0.6 0.7 multiply_add_fusion
  1.3 0.1 copy.17
  1.5 0.7 reshape.36.codes
  2.2 1.3 %reshape.38.egain = f32[1,896]{1,0:T(1,128)} reshape(f32[896]{0:T(1024)} %param.18) | data formatting | bytes 7168 | tf_op jit(solution)/shard_map/reshape | solution.py:727
  3.5 43.2 %fetch.1 = (bf16[12,12,8,896]{3,2,1,0:T(8,128)(2,1)}, bf16[384,256]{1,0:T(8,128)(2,1)}, bf16[384,256]{1,0:T(8,128)(2,1)}) custom-call(s32[384]{0:T(512)} %reshape.36.codes, bf16[8,12,8,896]{3,2,1,0:T(8,128)(2,1)} %bitcast.12, f32[1,896]{1,0:T(1,128)} %reshape.38.egain, bf16[896,1792]{1,0:T(8,128)(2,1)} %w_in.3, bf16[1792,896]{1,0:T(8,128)(2,1)} %w_out.3, ...), custom_call_target="tpu_custom_call" | custom-call | tf_op jit(solution)/shard_map/fetch/pallas_call | solution.py:249
  46.7 7.9 %attend.1 = (bf16[1152,896]{1,0:T(8,128)(2,1)}, bf16[384,256]{1,0:T(8,128)(2,1)}, bf16[384,256]{1,0:T(8,128)(2,1)}) custom-call(bf16[1152,896]{1,0:T(8,128)(2,1)} %bitcast.17, bf16[384,256]{1,0:T(8,128)(2,1)} %get-tuple-element.13.q, bf16[384,256]{1,0:T(8,128)(2,1)} %get-tuple-element.14.gctx, bf16[896,256]{1,0:T(8,128)(2,1)} %w_k.1, bf16[896,256]{1,0:T(8,128)(2,1)} %w_v.1), custom_call_target="tpu_custom_call" | custom-call | tf_op jit(solution)/shard_map/attend/pallas_call | solution.py:334
  54.6 1.9 %copy.18 = bf16[384,2048]{0,1:T(8,128)(2,1)S(1)} copy(bf16[384,2048]{1,0:T(8,128)(2,1)} %tok.1) | data formatting | bytes 3145728 | tf_op args[0]
  56.4 0.0 copy-start
  56.5 1.6 %copy.19 = bf16[384,8,256]{2,0,1:T(8,128)(2,1)} copy(bf16[384,8,256]{0,2,1:T(8,128)(2,1)S(1)} %bitcast.10) | data formatting | bytes 3145728 | tf_op jit(solution)/shard_map/reshape | solution.py:734
  58.1 0.0 copy-done
  58.1 0.5 copy.20
  58.6 1.3 %copy.21 = bf16[256,8,256]{2,0,1:T(8,128)(2,1)} copy(bf16[256,8,256]{0,2,1:T(8,128)(2,1)S(1)} %bitcast.15) | data formatting | bytes 2097152 | tf_op jit(solution)/shard_map/reshape | solution.py:735
  59.9 48.6 %give.1 = (bf16[32,2,8,896]{3,2,1,0:T(8,128)(2,1)}, bf16[2,384,256]{2,1,0:T(8,128)(2,1)}, bf16[2,2,384,256]{3,2,1,0:T(8,128)(2,1)}) custom-call(s32[384]{0:T(512)} %reshape.36.codes, bf16[12,12,8,896]{3,2,1,0:T(8,128)(2,1)} %bitcast.18, bf16[384,256]{1,0:T(8,128)(2,1)} %get-tuple-element.16.ctx, bf16[384,256]{1,0:T(8,128)(2,1)} %get-tuple-element.17.dq, ...), custom_call_target="tpu_custom_call" | custom-call | tf_op jit(solution)/shard_map/give/pallas_call | solution.py:615
  108.5 13.4 %settle.1 = (bf16[384,256]{1,0:T(8,128)(2,1)}, f32[384,256]{1,0:T(8,128)}, f32[8,12,896]{2,1,0:T(8,128)}) custom-call(s32[384]{0:T(512)} %reshape.36.codes, bf16[32,2,8,896]{3,2,1,0:T(8,128)(2,1)} %get-tuple-element.18.recv, bf16[2,384,256]{2,1,0:T(8,128)(2,1)} %get-tuple-element.19.own, bf16[2,2,384,256]{3,2,1,0:T(8,128)(2,1)} %get-tuple-element.20.fin, ...), custom_call_target="tpu_custom_call" | custom-call | tf_op jit(solution)/shard_map/settle/pallas_call | solution.py:695
  122.0 1.9 %copy.22 = f32[8,12,896]{2,0,1:T(8,128)} copy(f32[8,12,896]{2,1,0:T(8,128)} %get-tuple-element.26) | data formatting | bytes 688128 | tf_op jit(solution)/shard_map/settle/pallas_call | solution.py:695
Async XLA Ops:
  56.4 1.6 %copy-start = (bf16[256,2048]{1,0:T(8,128)(2,1)S(1)}, bf16[256,2048]{1,0:T(8,128)(2,1)}, u32[]{:S(2)}) copy-start(bf16[256,2048]{1,0:T(8,128)(2,1)} %w_p.1) | copy-start | bytes 3145732

commit v2 on v0

v2 whole, which is shorter than its diff:
```python
import functools

import jax
import jax.numpy as jnp
from jax import lax
from jax.experimental import pallas as pl
from jax.experimental.pallas import tpu as pltpu
from jax.sharding import Mesh
from jax.sharding import PartitionSpec as P

HD = 128
STRETCH = 64
K = 2
SEQ_LEN = 4096
UNIT = 8
EPSILON = 1e-06
MP = ("mp_0", "mp_1")
F32 = jnp.float32
BF16 = jnp.bfloat16
VM = pl.BlockSpec(memory_space=pltpu.VMEM)
SM = pl.BlockSpec(memory_space=pltpu.SMEM)
HB = pl.BlockSpec(memory_space=pltpu.HBM)
BIG = 64000 * 1024
FORE = (4, 3)
AFT = (3, 4)


def rcopy(src, dst, ssem, rsem, **where):
    return pltpu.make_async_remote_copy(
        src_ref=src,
        dst_ref=dst,
        send_sem=ssem,
        recv_sem=rsem,
        device_id=where,
        device_id_type=pl.DeviceIdType.MESH,
    )


def dot(a, b, ca=1, cb=0):
    return lax.dot_general(a, b, (((ca,), (cb,)), ((), ())), preferred_element_type=F32)


def rms_scaling(values):
    return lax.rsqrt(jnp.mean(values * values, axis=-1, keepdims=True) + EPSILON)


def sigmoid(v):
    return 1.0 / (1.0 + jnp.exp(-v))


def greet(n_seq, nx):
    me, x, c = lax.axis_index("seq"), lax.axis_index("mp_0"), lax.axis_index("mp_1")
    barrier = pltpu.get_barrier_semaphore()

    def tell(**where):
        pl.semaphore_signal(barrier, inc=1, device_id=where, device_id_type=pl.DeviceIdType.MESH)

    def far(k, carry):
        tell(seq=lax.rem(me + k, n_seq))
        return carry

    lax.fori_loop(1, n_seq, far, 0)
    tell(mp_0=lax.rem(x + 1, nx))
    tell(mp_0=lax.rem(x + nx - 1, nx))
    tell(mp_1=1 - c)
    return barrier, n_seq + 2


def seq_exchange(n_seq, n, src, dst, send, recv, src_lanes=None):
    me = lax.axis_index("seq")

    def piece(k, sending):
        peer = lax.rem(me + k, n_seq) if sending else lax.rem(me + n_seq - k, n_seq)
        at = me if sending else peer
        if src_lanes is None:
            a, b = src.at[peer, pl.ds(0, n)], dst.at[at, pl.ds(0, n)]
        else:
            a, b = src.at[peer, pl.ds(0, n), :, src_lanes], dst.at[at, pl.ds(0, n)]
        return rcopy(a, b, send.at[peer], recv.at[at], seq=peer)

    def run(sending, act):
        def go(k, carry):
            act(piece(k, sending))
            return carry

        lax.fori_loop(1, n_seq, go, 0)

    return (
        lambda: run(True, lambda copy: copy.start()),
        lambda: run(False, lambda copy: copy.wait_recv()),
        lambda: run(True, lambda copy: copy.wait_send()),
    )


def cuts(e, sizes):
    tiles = e // 128
    at, out = 0, []
    for i, share in enumerate(sizes):
        wide = tiles - at if i == len(sizes) - 1 else max(1, tiles * share // sum(sizes))
        out.append((at * 128, wide * 128))
        at += wide
    return out


def loop(count, f):
    def go(i, carry):
        f(i)
        return carry

    lax.fori_loop(0, count, go, 0)


def step_kernel(
    dims,
    shards, rows_in, db, egain, w_in, w_out, tok, gout, dgain, w_q, w_p, w_k, w_v,
    cca, gtok, gdb,
    win_v, w_in_v, w_out_v, tok_v, gout_v, w_q_v, w_p_v, w_k_v, w_v_v,
    enc, slope, outg, recvs, full, q, gctx, tscale, kv, ctx, dq, dkv,
    terms, sib, relay, last, comb, ge, back, got_back, acc, grad_hid,
    gn, outs, osib, orelay, ocomb, fin,
    rows_s, name_s, pick_s,
    lsem, a_send, a_recv, b_send, b_recv, d_send, d_recv, o_send, o_recv, e_send, e_recv, f_send, f_recv,
):
    n_seq, nx, nb, rows_dev, e, fore, aft = dims
    me, x, c = lax.axis_index("seq"), lax.axis_index("mp_0"), lax.axis_index("mp_1")
    barrier, greeted = greet(n_seq, nx)
    half = nb // 2
    per_dev = nb // K
    right, left, opp = lax.rem(x + 1, nx), lax.rem(x + nx - 1, nx), lax.rem(x + 2, nx)
    branches = (1, 2)

    def each(f, *args):
        for n in branches:
            @pl.when(c == n - 1)
            def _(n=n):
                f(n, *args)

    loads = [
        pltpu.make_async_copy(s, d, lsem.at[i])
        for i, (s, d) in enumerate(
            (
                (db.at[:, pl.ds(3 * x + c, 2)], win_v),
                (w_in, w_in_v),
                (w_out, w_out_v),
                (tok, tok_v),
                (w_q, w_q_v),
                (gout, gout_v),
                (w_p, w_p_v),
                (w_k, w_k_v),
                (w_v, w_v_v),
            )
        )
    ]
    for load in loads:
        load.start()

    def find(d):
        row, named = jnp.int32(0), jnp.int32(-1)
        for k in range(nb):
            hit = shards[k % K, d * per_dev + k // K] == me
            at = rows_in[k % K, d * per_dev + k // K]
            row, named = jnp.where(hit, at, row), jnp.where(hit, at, named)
        rows_s[d] = row
        name_s[d] = named

    loop(n_seq, find)

    units = rows_dev * 2 * UNIT
    loads[0].wait()
    values = win_v[...].astype(F32).reshape(units, e)
    gain = egain[...].reshape(1, e)
    normed = (values * rms_scaling(values) * gain).astype(BF16)
    loads[1].wait()
    pre = dot(normed, w_in_v[...])
    gate = sigmoid(pre)
    slope[...] = gate * (1.0 + pre * (1.0 - gate))
    hidden = (pre * gate).astype(BF16)
    loads[2].wait()
    encoded = values + dot(hidden, w_out_v[...])
    enc[...] = encoded.reshape(rows_dev, 2, UNIT, e).astype(BF16)

    def stage_out(d):
        outg[d] = enc[rows_s[d]]

    loop(n_seq, stage_out)
    for (l0, w), recv in zip(fore, recvs):
        recv[me] = outg[me, :, :, l0:l0 + w]
    pl.semaphore_wait(barrier, greeted)

    ask = {
        n: [
            seq_exchange(n_seq, n, outg, recv, a_send.at[i], a_recv.at[i], pl.ds(l0, w))
            for i, ((l0, w), recv) in enumerate(zip(fore, recvs))
        ]
        for n in branches
    }

    def ask_start(n):
        for plan in ask[n]:
            plan[0]()

    each(ask_start)

    size = min(128, q.shape[0])
    blocks = q.shape[0] // size
    loads[3].wait()
    loads[4].wait()

    def query(i):
        at = pl.ds(pl.multiple_of(i * size, size), size)
        vals = tok_v[at, :].astype(F32)
        scale = rms_scaling(vals)
        tscale[at, :] = scale
        q[at, :] = dot((vals * scale * dgain[...]).astype(BF16), w_q_v[...]).astype(BF16)

    loop(blocks, query)
    loads[5].wait()
    loads[6].wait()

    def context_grad(i):
        at = pl.ds(pl.multiple_of(i * size, size), size)
        where = me * q.shape[0] + i * size + lax.broadcasted_iota(jnp.int32, (size, 1), 0)
        alive = lax.rem(where // STRETCH, SEQ_LEN // STRETCH) != 0
        grad = dot(gout_v[at, :], w_p_v[...], 1, 1)
        gctx[at, :] = jnp.where(alive, grad, 0.0).astype(BF16)

    loop(blocks, context_grad)
    loads[7].wait()
    loads[8].wait()

    def mine(n, i, xx):
        l0, w = fore[i]
        return full.at[:, pl.ds(3 * xx + n - 1, n), :, pl.ds(l0, w)]

    def part(n, i, xx, h):
        l0, w = fore[i]
        return full.at[pl.ds(half * h, half), pl.ds(3 * xx + n - 1, n), :, pl.ds(l0, w)]

    def ring(n, i, k, ref, **where):
        return rcopy(ref, ref, b_send.at[i, k], b_recv.at[i, k], **where)

    def ring_copies(n, i):
        sib_to = dict(mp_1=1 - c)
        return [
            ring(n, i, 0, part(n, i, x, 0), mp_0=right),
            ring(n, i, 1, part(n, i, x, 1), mp_0=left),
            ring(n, i, 2, part(n, i, x, 1), mp_0=right),
            ring(n, i, 3, part(n, i, x, 0), mp_0=left),
            ring(n, i, 4, mine(n, i, x), **sib_to),
            ring(n, i, 5, part(n, i, left, 0), mp_0=right),
            ring(n, i, 6, part(n, i, right, 1), mp_0=left),
            ring(n, i, 7, mine(n, i, left), **sib_to),
            ring(n, i, 8, mine(n, i, right), **sib_to),
            ring(n, i, 9, part(n, i, opp, 0), **sib_to),
            ring(n, i, 10, part(n, i, opp, 1), **sib_to),
        ]

    def ring_got(n, i, k):
        ref = {
            0: lambda: part(n, i, left, 0),
            1: lambda: part(n, i, right, 1),
            2: lambda: part(n, i, left, 1),
            3: lambda: part(n, i, right, 0),
            4: lambda: mine(n, i, x),
            5: lambda: part(n, i, opp, 0),
            6: lambda: part(n, i, opp, 1),
            7: lambda: mine(n, i, left),
            8: lambda: mine(n, i, right),
            9: lambda: part(n, i, opp, 0),
            10: lambda: part(n, i, opp, 1),
        }[k]()
        ring(n, i, k, ref, mp_1=1 - c).wait_recv()

    def ring_open(n, i):
        ask[n][i][1]()
        l0, w = fore[i]

        def pick(j):
            slot = shards[lax.rem(j, K), me * per_dev + j // K]
            for u in range(n):
                full[j, 3 * x + n - 1 + u, :, l0:l0 + w] = recvs[i][slot, u]

        loop(nb, pick)
        for copy in ring_copies(n, i)[:5]:
            copy.start()

    def ring_pass(n, i):
        copies = ring_copies(n, i)
        ring_got(n, i, 0)
        copies[5].start()
        ring_got(n, i, 1)
        copies[6].start()
        ring_got(n, i, 2)
        copies[7].start()
        ring_got(n, i, 3)
        copies[8].start()

    def ring_close(n, i):
        copies = ring_copies(n, i)
        ring_got(n, i, 5)
        copies[9].start()
        ring_got(n, i, 6)
        copies[10].start()
        for k in (4, 7, 8, 9, 10):
            ring_got(3 - n, i, k)

    span = K * 12 * UNIT * nx // 4
    many = max(1, per_dev // 2)
    turns = per_dev // many
    tall = many * span

    def project(i):
        l0, w = fore[i]

        def go(t):
            at = pl.ds(pl.multiple_of(t * tall, tall), tall)
            rows = full[pl.ds(t * many * K, many * K), :, :, l0:l0 + w]
            rows = rows.astype(F32).reshape(tall, w).astype(BF16)
            for h, weight in enumerate((w_k_v, w_v_v)):
                out = dot(rows, weight[l0:l0 + w, :])
                if i:
                    out = out + kv[h, at, :]
                kv[h, at, :] = out

        loop(turns, go)

    each(ring_open, 0)
    for i in range(1, len(fore)):
        each(ring_pass, i - 1)
        each(ring_open, i)
        each(ring_close, i - 1)
        project(i - 1)
    each(ring_pass, len(fore) - 1)
    each(ring_close, len(fore) - 1)
    project(len(fore) - 1)

    width = q.shape[1]
    heads = width // HD
    factor = HD ** (-0.5)

    def attend(t):
        at = pl.ds(pl.multiple_of(t * tall, tall), tall)
        here = pl.ds(pl.multiple_of(t * many * STRETCH, many * STRETCH), many * STRETCH)
        todo = [(s, h) for s in range(many) for h in range(heads)]

        def pieces(block, high):
            return {
                (s, h): block[s * high:(s + 1) * high, h * HD:(h + 1) * HD] for s, h in todo
            }

        qs, gs = pieces(q[here, :], STRETCH), pieces(gctx[here, :], STRETCH)
        ks, vs = pieces(kv[0, at, :].astype(BF16), span), pieces(kv[1, at, :].astype(BF16), span)
        exps = {p: jnp.exp(dot(qs[p], ks[p], 1, 1) * factor) for p in todo}
        dps = {p: dot(gs[p], vs[p], 1, 1) for p in todo}
        probs = {p: exps[p] / jnp.sum(exps[p], axis=-1, keepdims=True) for p in todo}
        weights = {p: probs[p].astype(BF16) for p in todo}
        scores = {
            p: (
                probs[p] * (dps[p] - jnp.sum(probs[p] * dps[p], axis=-1, keepdims=True)) * factor
            ).astype(BF16)
            for p in todo
        }
        for s in range(many):
            lines = pl.ds(pl.multiple_of((t * many + s) * STRETCH, STRETCH), STRETCH)
            ends = pl.ds(pl.multiple_of((t * many + s) * span, span), span)
            for h in range(heads):
                p, lanes = (s, h), slice(h * HD, (h + 1) * HD)
                ctx[lines, lanes] = dot(weights[p], vs[p]).astype(BF16)
                dq[lines, lanes] = dot(scores[p], ks[p]).astype(BF16)
                dkv[0, ends, lanes] = dot(scores[p], qs[p], 0, 0).astype(BF16)
                dkv[1, ends, lanes] = dot(weights[p], gs[p], 0, 0).astype(BF16)

    loop(turns, attend)

    def lanes_of(i):
        l0, w = aft[i]
        return pl.ds(l0, w)

    def pair_copy(n, i, k, m):
        return rcopy(
            terms.at[:, pl.ds(3 * k + m - 1, m), :, lanes_of(i)],
            sib.at[k, :, pl.ds(0, m), :, lanes_of(i)],
            d_send.at[i, k],
            d_recv.at[i, k],
            mp_1=1 - c,
        )

    def pair_start(n, i):
        for k in range(nx):
            pair_copy(n, i, k, 3 - n).start()

    def relays(n, i):
        return [
            rcopy(
                comb.at[opp, pl.ds(half * h, half), pl.ds(0, n), :, lanes_of(i)],
                relay.at[h, :, pl.ds(0, n), :, lanes_of(i)],
                d_send.at[i, nx + h],
                d_recv.at[i, nx + h],
                mp_0=to,
            )
            for h, to in ((0, right), (1, left))
        ]

    def ends(n, i):
        return [
            rcopy(
                comb.at[to, :, pl.ds(0, n), :, lanes_of(i)],
                last.at[h, :, pl.ds(0, n), :, lanes_of(i)],
                d_send.at[i, nx + 2 + h],
                d_recv.at[i, nx + 2 + h],
                mp_0=to,
            )
            for h, to in ((0, right), (1, left))
        ]

    def reduce_pair(n, i):
        l0, w = aft[i]
        for k in range(nx):
            pair_copy(n, i, k, n).wait_recv()

        def add(k, j):
            for u in range(n):
                comb[k, j, u, :, l0:l0 + w] = (
                    terms[j, 3 * k + n - 1 + u, :, l0:l0 + w].astype(F32)
                    + sib[k, j, u, :, l0:l0 + w].astype(F32)
                ).astype(BF16)

        loop(nb, lambda j: add(opp, j))
        for copy in relays(n, i):
            copy.start()
        for k in (right, left, x):
            loop(nb, lambda j, k=k: add(k, j))

    def reduce_ends(n, i):
        l0, w = aft[i]
        for h, (copy, to) in enumerate(zip(relays(n, i), (right, left))):
            copy.wait_recv()

            def add(j, h=h, to=to):
                for u in range(n):
                    comb[to, half * h + j, u, :, l0:l0 + w] = (
                        comb[to, half * h + j, u, :, l0:l0 + w].astype(F32)
                        + relay[h, j, u, :, l0:l0 + w].astype(F32)
                    ).astype(BF16)

            loop(half, add)
            ends(n, i)[h].start()

    def give_back(n, i):
        l0, w = aft[i]
        for copy in ends(n, i):
            copy.wait_recv()

        def add(j):
            for u in range(n):
                ge[j, u, :, l0:l0 + w] = (
                    comb[x, j, u, :, l0:l0 + w].astype(F32)
                    + last[0, j, u, :, l0:l0 + w].astype(F32)
                    + last[1, j, u, :, l0:l0 + w].astype(F32)
                ).astype(BF16)

        loop(nb, add)

        def stage(s):
            spot = pick_s[s]
            for u in range(n):
                back[i][s, u] = ge[spot, u, :, l0:l0 + w]

        loop(n_seq, stage)
        for u in range(n):
            got_back[i][me, u] = back[i][me, u]
        returns[n][i][0]()

    returns = {
        n: [
            seq_exchange(n_seq, n, back[i], got_back[i], e_send.at[i], e_recv.at[i])
            for i in range(len(aft))
        ]
        for n in branches
    }

    def shared(i):
        return rcopy(
            got_back[i].at[:, 0], got_back[i].at[:, 1], f_send.at[i], f_recv.at[i], mp_1=1 - c
        )

    def terms_of(i):
        l0, w = aft[i]

        def go(t):
            at = pl.ds(pl.multiple_of(t * tall, tall), tall)
            out = dot(dkv[0, at, :], w_k_v[l0:l0 + w, :], 1, 1)
            out = out + dot(dkv[1, at, :], w_v_v[l0:l0 + w, :], 1, 1)
            terms[pl.ds(t * many * K, many * K), :, :, l0:l0 + w] = out.reshape(
                many * K, 3 * nx, UNIT, w
            ).astype(BF16)

        loop(turns, go)

    def find_back(s):
        spot = jnp.int32(0)
        for k in range(nb):
            spot = jnp.where(shards[k % K, me * per_dev + k // K] == s, k, spot)
        pick_s[s] = spot

    high = ctx.shape[0]
    lanes = 2 * nx
    cols = tok_v.shape[1] // lanes
    live = lax.rem(
        (me * high + lax.broadcasted_iota(jnp.int32, (high, 1), 0)) // STRETCH, SEQ_LEN // STRETCH
    ) != 0

    def columns(l):
        return pl.ds(pl.multiple_of(l * cols, cols), cols)

    def out_terms():
        def forward(l, total):
            out = dot(ctx[...], w_p_v[:, columns(l)])
            outs[l // 2, lax.rem(l, 2), 0] = jnp.where(live, out, 0.0).astype(BF16)
            grad = dot(dq[...], w_q_v[columns(l), :], 1, 1) * dgain[:, columns(l)]
            gn[l] = grad
            return total + jnp.sum(
                grad * tok_v[:, columns(l)].astype(F32), axis=-1, keepdims=True
            )

        total = lax.fori_loop(0, lanes, forward, jnp.zeros((high, 1), F32))
        scale = tscale[...]
        tilt = total * scale * scale / (lanes * cols)

        def finish(l):
            grad = scale * (gn[l] - tok_v[:, columns(l)].astype(F32) * tilt)
            outs[l // 2, lax.rem(l, 2), 1] = grad.astype(BF16)

        loop(lanes, finish)

    def out_pair():
        return [
            rcopy(outs.at[k, 1 - c], osib.at[k], o_send.at[k], o_recv.at[k], mp_1=1 - c)
            for k in range(nx)
        ]

    def out_relays():
        return [
            rcopy(ocomb.at[opp, h], orelay.at[h], o_send.at[nx + h], o_recv.at[nx + h], mp_0=to)
            for h, to in ((0, right), (1, left))
        ]

    def out_ends():
        return [
            rcopy(ocomb.at[to], fin.at[h], o_send.at[nx + 2 + h], o_recv.at[nx + 2 + h], mp_0=to)
            for h, to in ((0, right), (1, left))
        ]

    def by_stretch(f):
        loop(high // STRETCH, lambda i: f(pl.ds(pl.multiple_of(i * STRETCH, STRETCH), STRETCH)))

    def out_reduce_pair():
        for copy in out_pair():
            copy.wait_recv()

        def add(k):
            def go(at):
                for t in range(2):
                    ocomb[k, t, at, :] = (
                        outs[k, c, t, at, :].astype(F32) + osib[k, t, at, :].astype(F32)
                    ).astype(BF16)

            by_stretch(go)

        add(opp)
        for copy in out_relays():
            copy.start()
        for k in (right, left, x):
            add(k)

    def out_reduce_ends():
        for h, (copy, to) in enumerate(zip(out_relays(), (right, left))):
            copy.wait_recv()

            def go(at, h=h, to=to):
                ocomb[to, h, at, :] = (
                    ocomb[to, h, at, :].astype(F32) + orelay[h, at, :].astype(F32)
                ).astype(BF16)

            by_stretch(go)
            out_ends()[h].start()

    def out_close():
        for copy in out_ends():
            copy.wait_recv()

        def go(at):
            def total(t):
                return (
                    ocomb[x, t, at, :].astype(F32)
                    + fin[0, t, at, :].astype(F32)
                    + fin[1, t, at, :].astype(F32)
                )

            cca[at, :] = total(0).astype(BF16)
            gtok[at, :] = total(1)

        by_stretch(go)

    for i in range(len(aft)):
        terms_of(i)
        each(pair_start, i)
    loop(n_seq, find_back)
    each(reduce_pair, 0)
    out_terms()
    for copy in out_pair():
        copy.start()
    for i in range(1, len(aft)):
        each(reduce_pair, i)
    each(reduce_ends, 0)
    out_reduce_pair()
    for i in range(1, len(aft)):
        each(reduce_ends, i)
    for i in range(len(aft)):
        each(give_back, i)
        if i == 0:
            out_reduce_ends()

    def collect(n, i):
        returns[n][i][1]()
        if n == 2:
            shared(i).start()
        else:
            shared(i).wait_recv()

    def tally(i):
        l0, w = aft[i]
        for u in range(2):
            def add(d, sums):
                named = name_s[d]
                slot = got_back[i][d, u].astype(F32)
                return tuple(
                    total + jnp.where(named == r, slot, 0.0) for r, total in enumerate(sums)
                )

            sums = lax.fori_loop(
                0, n_seq, add, tuple(jnp.zeros((UNIT, w), F32) for _ in range(rows_dev))
            )
            for r in range(rows_dev):
                acc[r, u, :, l0:l0 + w] = sums[r]
        part = acc[:, :, :, l0:l0 + w].reshape(units, w).astype(BF16)
        out = dot(part, w_out_v[:, l0:l0 + w], 1, 1)
        grad_hid[...] = out if i == 0 else grad_hid[...] + out

    for i in range(len(aft)):
        each(collect, i)
        if i == len(aft) - 1:
            out_close()
        tally(i)

    values = win_v[...].astype(F32).reshape(units, e)
    scaling = rms_scaling(values)
    unit = values * scaling
    g = dot((grad_hid[...] * slope[...]).astype(BF16), w_in_v[...], 1, 1) * egain[...].reshape(1, e)
    grad_enc = acc[...].reshape(units, e)
    out = grad_enc + scaling * (g - unit * jnp.mean(g * unit, axis=-1, keepdims=True))
    out = out.reshape(rows_dev, 2 * UNIT, e)
    keep = gdb.shape[0]
    for n in range(2):
        @pl.when(c == n)
        def _(n=n):
            at = (2 * UNIT - keep) * n
            gdb[...] = jnp.swapaxes(out[:, at:at + keep, :], 0, 1)

    def drain(n):
        for i in range(len(fore)):
            ask[n][i][2]()
            for copy in ring_copies(n, i):
                copy.wait_send()
        for i in range(len(aft)):
            returns[n][i][2]()
            for k in range(nx):
                pair_copy(n, i, k, 3 - n).wait_send()
            for copy in relays(n, i) + ends(n, i):
                copy.wait_send()
            if n == 2:
                shared(i).wait_send()

    each(drain)
    for copy in out_pair() + out_relays() + out_ends():
        copy.wait_send()


def step(dims, *args):
    n_seq, nx, nb, rows_dev, e, fore, aft = dims
    shards, rows_in, db, egain, w_in, w_out, tok, gout, dgain, w_q, w_p, w_k, w_v = args
    slot = (2, UNIT, e)
    high, width = tok.shape[0], w_q.shape[1]
    lanes = 2 * nx
    cols = tok.shape[1] // lanes
    half = nb // 2
    units = rows_dev * 2 * UNIT
    rows = nb * 3 * nx * UNIT
    nf, na = len(fore), len(aft)
    dma = pltpu.SemaphoreType.DMA
    return pl.pallas_call(
        functools.partial(step_kernel, dims),
        out_shape=(
            jax.ShapeDtypeStruct((high, cols), BF16),
            jax.ShapeDtypeStruct((high, cols), F32),
            jax.ShapeDtypeStruct((3 * UNIT // 2, rows_dev, e), F32),
        ),
        in_specs=[SM, SM, HB, VM, HB, HB, HB, HB, VM, HB, HB, HB, HB],
        out_specs=(VM, VM, VM),
        scratch_shapes=[
            pltpu.VMEM((rows_dev, *slot), BF16),
            *[pltpu.VMEM(a.shape, BF16) for a in (w_in, w_out, tok, gout, w_q, w_p, w_k, w_v)],
            pltpu.VMEM((rows_dev, *slot), BF16),
            pltpu.VMEM((units, w_in.shape[1]), F32),
            pltpu.VMEM((n_seq, *slot), BF16),
            [pltpu.VMEM((n_seq, 2, UNIT, w), BF16) for _, w in fore],
            pltpu.VMEM((nb, 3 * nx, UNIT, e), BF16),
            pltpu.VMEM((high, width), BF16),
            pltpu.VMEM((high, width), BF16),
            pltpu.VMEM((high, 1), F32),
            pltpu.VMEM((2, rows, width), F32),
            pltpu.VMEM((high, width), BF16),
            pltpu.VMEM((high, width), BF16),
            pltpu.VMEM((2, rows, width), BF16),
            pltpu.VMEM((nb, 3 * nx, UNIT, e), BF16),
            pltpu.VMEM((nx, nb, *slot), BF16),
            pltpu.VMEM((2, half, *slot), BF16),
            pltpu.VMEM((2, nb, *slot), BF16),
            pltpu.VMEM((nx, nb, *slot), BF16),
            pltpu.VMEM((nb, *slot), BF16),
            [pltpu.VMEM((n_seq, 2, UNIT, w), BF16) for _, w in aft],
            [pltpu.VMEM((n_seq, 2, UNIT, w), BF16) for _, w in aft],
            pltpu.VMEM((rows_dev, *slot), F32),
            pltpu.VMEM((units, w_in.shape[1]), F32),
            pltpu.VMEM((lanes, high, cols), F32),
            pltpu.VMEM((nx, 2, 2, high, cols), BF16),
            pltpu.VMEM((nx, 2, high, cols), BF16),
            pltpu.VMEM((2, high, cols), BF16),
            pltpu.VMEM((nx, 2, high, cols), BF16),
            pltpu.VMEM((2, 2, high, cols), BF16),
            pltpu.SMEM((n_seq,), jnp.int32),
            pltpu.SMEM((n_seq,), jnp.int32),
            pltpu.SMEM((n_seq,), jnp.int32),
            dma((9,)),
            dma((nf, n_seq)),
            dma((nf, n_seq)),
            dma((nf, 11)),
            dma((nf, 11)),
            dma((na, nx + 4)),
            dma((na, nx + 4)),
            dma((nx + 4,)),
            dma((nx + 4,)),
            dma((na, n_seq)),
            dma((na, n_seq)),
            dma((na,)),
            dma((na,)),
        ],
        compiler_params=pltpu.CompilerParams(
            collective_id=0, has_side_effects=True, vmem_limit_bytes=BIG
        ),
        name="step",
    )(*args)


def body(
    n_seq, nx,
    tokens, database, nb_shard, nb_row, dec_gain, enc_gain,
    w_in, w_out, w_query, w_key, w_value, w_proj, grad_out,
):
    rows_dev, length, e = database.shape
    nb = tokens.shape[0] // STRETCH * K
    dims = (n_seq, nx, nb, rows_dev, e, cuts(e, FORE), cuts(e, AFT))
    cca, gtok, gdb = step(
        dims, nb_shard.T, nb_row.T, database.reshape(rows_dev, length // UNIT, UNIT, e), enc_gain,
        w_in, w_out, tokens, grad_out, dec_gain.reshape(1, -1), w_query, w_proj, w_key, w_value,
    )
    return cca, gtok, jnp.swapaxes(gdb, 0, 1)


def solution(mesh):
    n_seq = mesh.shape["seq"]
    nx = mesh.shape["mp"] // 2
    split = Mesh(mesh.devices.reshape(n_seq, nx, 2), ("seq", "mp_0", "mp_1"))
    placed = (
        P("seq", None),
        P("seq", None, None),
        P(),
        P(),
        P(),
        P(),
        P(),
        P(),
        P(None, MP),
        P(None, MP),
        P(None, MP),
        P(MP, None),
        P("seq", None),
    )
    return jax.shard_map(
        functools.partial(body, n_seq, nx),
        mesh=split,
        in_specs=placed,
        out_specs=(P("seq", MP), P("seq", MP), P("seq", MP, None)),
        check_vma=False,
    )
```

time: 252 us -> 91 us (0.36); the launches traced: 248 us -> 89.7 us
  blocking collectives: 105 us -> 0 us
  Pallas kernels: 0 us -> 84 us
  matrix products: 44.9 us -> 0 us
  local copies, waits for them, and re-layouts: 41 us -> 5.11 us
  other arithmetic: 17.9 us -> 0 us
  between operations: 14.4 us -> 0.64 us
  waiting for transfers between devices: 12.6 us -> 0 us
  starting transfers between devices: 12.3 us -> 0 us
    pallas_call x0 -> x1, Pallas kernels: none -> 84 us  [step(): pl.pallas_call(functools.partial(step_kernel, dims), out_shape=(jax.Shape...]
    all_to_all x2 -> x0, blocking collectives: 66.4 us -> none  [the longest x1 38.6 us: summed_on_arrival(): tiles = lax.all_to_all(split_up(x, dim, devices), axis, 0, 0, tiled=True)]
    dot_general x18 -> x0, matrix products: 42.2 us -> none  [the longest x1 6.08 us: encode_back(): jnp.einsum('nlf,ef->nle', grad_pre, w_in, preferred_element_type=jnp.floa...]
    all_gather x4 -> x0, blocking collectives: 38.5 us -> none  [gather_in_order(): tiles = lax.all_gather(tiles, axes[k], axis=0, tiled=True)]
    reshape x10 -> x0, local copies, waits for them, and re-layouts: 21.4 us -> none  [the longest x1 4.64 us: joined_along(): return jnp.moveaxis(tiles, 0, dim).reshape(shape)]
    all_to_all x1 -> x0, waiting for transfers between devices: 12.6 us -> none  [body(): lax.all_to_all(outgoing, 'seq', split_axis=0, concat_axis=0, tiled=True)]
    all_to_all x1 -> x0, starting transfers between devices: 12.3 us -> none  [body(): lax.all_to_all(outgoing, 'seq', split_axis=0, concat_axis=0, tiled=True)]
    convert_element_type x5 -> x0, local copies, waits for them, and re-layouts: 7.62 us -> none  [the longest x1 2.5 us: body(): grad_key = jnp.einsum('chqk,cqhd->ckhd', grad_score, query_blk, preferred...]
  transfers between devices with their start and end apart: 2 -> 0, of which waited for: 1 -> 0; matrix products, arithmetic and copies ran while one was open for 20% -> 0% of each run, Pallas kernels for 0% -> 0%
where the time goes in v2:
time: 91 us; the launch traced here: 89.7 us
  Pallas kernels  84 us (92%)
  local copies, waits for them, and re-layouts  5.11 us (6%)
    pallas_call x1, Pallas kernels, step(): pl.pallas_call(functools.partial(step_kernel, dims), out_shape=(jax.Shape...  84 us
    unnamed x3, local copies, waits for them, and re-layouts  5.11 us

profile of v2, /device:TPU:1, one launch (start us, length us, event | category | flops | bytes accessed | tf_op | source)
XLA Modules:
  0.0 89.7 jit_solution(12829424221074254500)
XLA Ops:
  0.6 84.0 %step.1 = (bf16[384,256]{1,0:T(8,128)(2,1)}, f32[384,256]{1,0:T(8,128)}, f32[12,8,896]{2,1,0:T(8,128)}) custom-call(s32[2,192]{1,0:T(2,128)} %bitcast.8, s32[2,192]{1,0:T(2,128)} %bitcast.9, bf16[8,12,8,896]{3,2,1,0:T(8,128)(2,1)} %bitcast.5, f32[896]{0:T(1024)} %egain.1, bf16[896,1792]{1,0:T(8,128)(2,1)} %w_in.1, bf16[1792,896]{1,0:T(8,128)(2,1)} %w_out.1, ...), custom_call_target="tpu_custom_call" | custom-call | tf_op jit(solution)/shard_map/step/pallas_call | solution.py:701
  84.6 1.6 %copy.19 = bf16[384,256]{1,0:T(8,128)(2,1)} copy(bf16[384,256]{1,0:T(8,128)(2,1)} %get-tuple-element.12) | data formatting | bytes 393216
  86.2 1.8 %copy.20 = f32[384,256]{1,0:T(8,128)} copy(f32[384,256]{1,0:T(8,128)} %get-tuple-element.13) | data formatting | bytes 786432
  88.0 1.7 %copy.21 = f32[8,12,896]{2,0,1:T(8,128)} copy(f32[8,12,896]{2,0,1:T(8,128)} %bitcast.6) | data formatting | bytes 688128

commit v3 on v2

--- a/solution.py
+++ b/solution.py
@@ -20,9 +20,9 @@
 VM = pl.BlockSpec(memory_space=pltpu.VMEM)
 SM = pl.BlockSpec(memory_space=pltpu.SMEM)
 HB = pl.BlockSpec(memory_space=pltpu.HBM)
-BIG = 64000 * 1024
-FORE = (4, 3)
-AFT = (3, 4)
+BIG = 46000 * 1024
+FORE = (4, 2, 1)
+AFT = (2, 3, 2)
 
 
 def rcopy(src, dst, ssem, rsem, **where):
@@ -123,7 +123,6 @@
 ):
     n_seq, nx, nb, rows_dev, e, fore, aft = dims
     me, x, c = lax.axis_index("seq"), lax.axis_index("mp_0"), lax.axis_index("mp_1")
-    barrier, greeted = greet(n_seq, nx)
     half = nb // 2
     per_dev = nb // K
     right, left, opp = lax.rem(x + 1, nx), lax.rem(x + nx - 1, nx), lax.rem(x + 2, nx)
@@ -151,8 +150,9 @@
             )
         )
     ]
-    for load in loads:
+    for load in loads[:3]:
         load.start()
+    barrier, greeted = greet(n_seq, nx)
 
     def find(d):
         row, named = jnp.int32(0), jnp.int32(-1)
@@ -176,6 +176,8 @@
     slope[...] = gate * (1.0 + pre * (1.0 - gate))
     hidden = (pre * gate).astype(BF16)
     loads[2].wait()
+    for load in loads[3:]:
+        load.start()
     encoded = values + dot(hidden, w_out_v[...])
     enc[...] = encoded.reshape(rows_dev, 2, UNIT, e).astype(BF16)
 
@@ -386,70 +388,74 @@
         )
 
     def pair_start(n, i):
-        for k in range(nx):
+        for k in (opp, left, right, x):
             pair_copy(n, i, k, 3 - n).start()
 
-    def relays(n, i):
-        return [
-            rcopy(
-                comb.at[opp, pl.ds(half * h, half), pl.ds(0, n), :, lanes_of(i)],
-                relay.at[h, :, pl.ds(0, n), :, lanes_of(i)],
-                d_send.at[i, nx + h],
-                d_recv.at[i, nx + h],
-                mp_0=to,
-            )
-            for h, to in ((0, right), (1, left))
-        ]
-
-    def ends(n, i):
-        return [
-            rcopy(
-                comb.at[to, :, pl.ds(0, n), :, lanes_of(i)],
-                last.at[h, :, pl.ds(0, n), :, lanes_of(i)],
-                d_send.at[i, nx + 2 + h],
-                d_recv.at[i, nx + 2 + h],
-                mp_0=to,
-            )
-            for h, to in ((0, right), (1, left))
-        ]
+    toward = (right, left)
+
+    def piece(n, i, k, h, to, dst, sem):
+        return rcopy(
+            comb.at[k, pl.ds(half * h, half), pl.ds(0, n), :, lanes_of(i)],
+            dst.at[:, pl.ds(0, n), :, lanes_of(i)],
+            d_send.at[i, sem],
+            d_recv.at[i, sem],
+            mp_0=to,
+        )
+
+    def relay_of(n, i, h):
+        return piece(n, i, opp, h, toward[h], relay.at[h], nx + h)
+
+    def plain_of(n, i, h):
+        to = toward[1 - h]
+        return piece(n, i, to, h, to, last.at[1 - h, pl.ds(half * h, half)], nx + 2 + h)
+
+    def final_of(n, i, h):
+        to = toward[h]
+        return piece(n, i, to, h, to, last.at[h, pl.ds(half * h, half)], nx + 4 + h)
 
     def reduce_pair(n, i):
         l0, w = aft[i]
-        for k in range(nx):
+
+        def add(k):
             pair_copy(n, i, k, n).wait_recv()
 
-        def add(k, j):
-            for u in range(n):
-                comb[k, j, u, :, l0:l0 + w] = (
-                    terms[j, 3 * k + n - 1 + u, :, l0:l0 + w].astype(F32)
-                    + sib[k, j, u, :, l0:l0 + w].astype(F32)
-                ).astype(BF16)
-
-        loop(nb, lambda j: add(opp, j))
-        for copy in relays(n, i):
-            copy.start()
-        for k in (right, left, x):
-            loop(nb, lambda j, k=k: add(k, j))
+            def go(j):
+                for u in range(n):
+                    comb[k, j, u, :, l0:l0 + w] = (
+                        terms[j, 3 * k + n - 1 + u, :, l0:l0 + w].astype(F32)
+                        + sib[k, j, u, :, l0:l0 + w].astype(F32)
+                    ).astype(BF16)
+
+            loop(nb, go)
+
+        add(opp)
+        for h in range(2):
+            relay_of(n, i, h).start()
+        for h in range(2):
+            add(toward[1 - h])
+            plain_of(n, i, h).start()
+        add(x)
 
     def reduce_ends(n, i):
         l0, w = aft[i]
-        for h, (copy, to) in enumerate(zip(relays(n, i), (right, left))):
-            copy.wait_recv()
-
-            def add(j, h=h, to=to):
+        for h in range(2):
+            relay_of(n, i, h).wait_recv()
+
+            def add(j, h=h):
                 for u in range(n):
-                    comb[to, half * h + j, u, :, l0:l0 + w] = (
-                        comb[to, half * h + j, u, :, l0:l0 + w].astype(F32)
+                    comb[toward[h], half * h + j, u, :, l0:l0 + w] = (
+                        comb[toward[h], half * h + j, u, :, l0:l0 + w].astype(F32)
                         + relay[h, j, u, :, l0:l0 + w].astype(F32)
                     ).astype(BF16)
 
             loop(half, add)
-            ends(n, i)[h].start()
+            final_of(n, i, h).start()
 
     def give_back(n, i):
         l0, w = aft[i]
-        for copy in ends(n, i):
-            copy.wait_recv()
+        for h in range(2):
+            plain_of(n, i, h).wait_recv()
+            final_of(n, i, h).wait_recv()
 
         def add(j):
             for u in range(n):
@@ -514,16 +520,21 @@
         return pl.ds(pl.multiple_of(l * cols, cols), cols)
 
     def out_terms():
-        def forward(l, total):
+        def forward(l):
             out = dot(ctx[...], w_p_v[:, columns(l)])
             outs[l // 2, lax.rem(l, 2), 0] = jnp.where(live, out, 0.0).astype(BF16)
+
+        loop(lanes, forward)
+
+    def grad_terms():
+        def backward(l, total):
             grad = dot(dq[...], w_q_v[columns(l), :], 1, 1) * dgain[:, columns(l)]
             gn[l] = grad
             return total + jnp.sum(
                 grad * tok_v[:, columns(l)].astype(F32), axis=-1, keepdims=True
             )
 
-        total = lax.fori_loop(0, lanes, forward, jnp.zeros((high, 1), F32))
+        total = lax.fori_loop(0, lanes, backward, jnp.zeros((high, 1), F32))
         scale = tscale[...]
         tilt = total * scale * scale / (lanes * cols)
 
@@ -533,93 +544,96 @@
 
         loop(lanes, finish)
 
-    def out_pair():
-        return [
-            rcopy(outs.at[k, 1 - c], osib.at[k], o_send.at[k], o_recv.at[k], mp_1=1 - c)
-            for k in range(nx)
-        ]
-
-    def out_relays():
-        return [
-            rcopy(ocomb.at[opp, h], orelay.at[h], o_send.at[nx + h], o_recv.at[nx + h], mp_0=to)
-            for h, to in ((0, right), (1, left))
-        ]
-
-    def out_ends():
-        return [
-            rcopy(ocomb.at[to], fin.at[h], o_send.at[nx + 2 + h], o_recv.at[nx + 2 + h], mp_0=to)
-            for h, to in ((0, right), (1, left))
-        ]
+    def out_pair(k, h):
+        return rcopy(
+            outs.at[k, 1 - c, h], osib.at[k, h], o_send.at[h, k], o_recv.at[h, k], mp_1=1 - c
+        )
+
+    def out_piece(k, h, to, dst, sem):
+        return rcopy(ocomb.at[k, h], dst, o_send.at[h, sem], o_recv.at[h, sem], mp_0=to)
+
+    def out_relay(h):
+        return out_piece(opp, h, toward[h], orelay.at[h], nx)
+
+    def out_plain(h):
+        to = toward[1 - h]
+        return out_piece(to, h, to, fin.at[1 - h, h], nx + 1)
+
+    def out_final(h):
+        to = toward[h]
+        return out_piece(to, h, to, fin.at[h, h], nx + 2)
+
+    def out_open(h):
+        for k in (opp, left, right, x):
+            out_pair(k, h).start()
 
     def by_stretch(f):
         loop(high // STRETCH, lambda i: f(pl.ds(pl.multiple_of(i * STRETCH, STRETCH), STRETCH)))
 
-    def out_reduce_pair():
-        for copy in out_pair():
-            copy.wait_recv()
-
+    def out_reduce_pair(h):
         def add(k):
+            out_pair(k, h).wait_recv()
+
             def go(at):
-                for t in range(2):
-                    ocomb[k, t, at, :] = (
-                        outs[k, c, t, at, :].astype(F32) + osib[k, t, at, :].astype(F32)
-                    ).astype(BF16)
+                ocomb[k, h, at, :] = (
+                    outs[k, c, h, at, :].astype(F32) + osib[k, h, at, :].astype(F32)
+                ).astype(BF16)
 
             by_stretch(go)
 
         add(opp)
-        for copy in out_relays():
-            copy.start()
-        for k in (right, left, x):
-            add(k)
-
-    def out_reduce_ends():
-        for h, (copy, to) in enumerate(zip(out_relays(), (right, left))):
-            copy.wait_recv()
-
-            def go(at, h=h, to=to):
-                ocomb[to, h, at, :] = (
-                    ocomb[to, h, at, :].astype(F32) + orelay[h, at, :].astype(F32)
-                ).astype(BF16)
-
-            by_stretch(go)
-            out_ends()[h].start()
-
-    def out_close():
-        for copy in out_ends():
-            copy.wait_recv()
+        out_relay(h).start()
+        add(toward[1 - h])
+        out_plain(h).start()
+        add(toward[h])
+        add(x)
+
+    def out_reduce_ends(h):
+        out_relay(h).wait_recv()
 
         def go(at):
-            def total(t):
-                return (
-                    ocomb[x, t, at, :].astype(F32)
-                    + fin[0, t, at, :].astype(F32)
-                    + fin[1, t, at, :].astype(F32)
-                )
-
-            cca[at, :] = total(0).astype(BF16)
-            gtok[at, :] = total(1)
+            ocomb[toward[h], h, at, :] = (
+                ocomb[toward[h], h, at, :].astype(F32) + orelay[h, at, :].astype(F32)
+            ).astype(BF16)
 
         by_stretch(go)
-
-    for i in range(len(aft)):
+        out_final(h).start()
+
+    def out_close(h, target):
+        out_plain(h).wait_recv()
+        out_final(h).wait_recv()
+
+        def go(at):
+            total = ocomb[x, h, at, :].astype(F32) + fin[0, h, at, :].astype(F32)
+            target[at, :] = (total + fin[1, h, at, :].astype(F32)).astype(target.dtype)
+
+        by_stretch(go)
+
+    m = len(aft)
+    for i in range(m):
         terms_of(i)
         each(pair_start, i)
     loop(n_seq, find_back)
+    out_terms()
+    out_open(0)
     each(reduce_pair, 0)
-    out_terms()
-    for copy in out_pair():
-        copy.start()
-    for i in range(1, len(aft)):
+    each(reduce_pair, 1)
+    grad_terms()
+    out_open(1)
+    each(reduce_ends, 0)
+    for i in range(2, m):
         each(reduce_pair, i)
-    each(reduce_ends, 0)
-    out_reduce_pair()
-    for i in range(1, len(aft)):
+    out_reduce_pair(0)
+    each(reduce_ends, 1)
+    each(give_back, 0)
+    for i in range(2, m):
         each(reduce_ends, i)
-    for i in range(len(aft)):
+    out_reduce_pair(1)
+    each(give_back, 1)
+    out_reduce_ends(0)
+    for i in range(2, m):
         each(give_back, i)
-        if i == 0:
-            out_reduce_ends()
+    out_reduce_ends(1)
 
     def collect(n, i):
         returns[n][i][1]()
@@ -649,9 +663,10 @@
 
     for i in range(len(aft)):
         each(collect, i)
-        if i == len(aft) - 1:
-            out_close()
         tally(i)
+        if i == m - 2:
+            out_close(0, cca)
+            out_close(1, gtok)
 
     values = win_v[...].astype(F32).reshape(units, e)
     scaling = rms_scaling(values)
@@ -676,14 +691,16 @@
             returns[n][i][2]()
             for k in range(nx):
                 pair_copy(n, i, k, 3 - n).wait_send()
-            for copy in relays(n, i) + ends(n, i):
-                copy.wait_send()
+            for h in range(2):
+                for copy in (relay_of(n, i, h), plain_of(n, i, h), final_of(n, i, h)):
+                    copy.wait_send()
             if n == 2:
                 shared(i).wait_send()
 
     each(drain)
-    for copy in out_pair() + out_relays() + out_ends():
-        copy.wait_send()
+    for h in range(2):
+        for copy in [out_pair(k, h) for k in range(nx)] + [out_relay(h), out_plain(h), out_final(h)]:
+            copy.wait_send()
 
 
 def step(dims, *args):
@@ -746,10 +763,10 @@
             dma((nf, n_seq)),
             dma((nf, 11)),
             dma((nf, 11)),
-            dma((na, nx + 4)),
-            dma((na, nx + 4)),
-            dma((nx + 4,)),
-            dma((nx + 4,)),
+            dma((na, nx + 6)),
+            dma((na, nx + 6)),
+            dma((2, nx + 3)),
+            dma((2, nx + 3)),
             dma((na, n_seq)),
             dma((na, n_seq)),
             dma((na,)),
@@ -759,7 +776,7 @@
             collective_id=0, has_side_effects=True, vmem_limit_bytes=BIG
         ),
         name="step",
-    )(*args)
+    )(*[pltpu.with_memory_space_constraint(a, pltpu.HBM) for a in args])
 
 
 def body(

time: 91 us -> 94.8 us (1.042); the launches traced: 89.7 us -> 94.7 us
  Pallas kernels: 84 us -> 91.9 us
  local copies, waits for them, and re-layouts: 5.11 us -> 2.15 us
    pallas_call x1, Pallas kernels: 84 us -> 91.9 us  [step(): pl.pallas_call(functools.partial(step_kernel, dims), out_shape=(jax.Shape...]
    unnamed x3, local copies, waits for them, and re-layouts: 5.11 us -> 2.15 us
where the time goes in v3:
time: 94.8 us; the launch traced here: 94.7 us
  Pallas kernels  91.9 us (97%)
  local copies, waits for them, and re-layouts  2.15 us (2%)
    pallas_call x1, Pallas kernels, step(): pl.pallas_call(functools.partial(step_kernel, dims), out_shape=(jax.Shape...  91.9 us
    unnamed x3, local copies, waits for them, and re-layouts  2.15 us

profile of v3, /device:TPU:1, one launch (start us, length us, event | category | flops | bytes accessed | tf_op | source)
XLA Modules:
  0.0 94.7 jit_solution(9700388373369725192)
XLA Ops:
  0.6 91.9 %step.1 = (bf16[384,256]{1,0:T(8,128)(2,1)S(1)}, f32[384,256]{1,0:T(8,128)S(1)}, f32[12,8,896]{2,1,0:T(8,128)S(1)}) custom-call(s32[2,192]{1,0:T(2,128)} %bitcast.8, s32[2,192]{1,0:T(2,128)} %bitcast.9, bf16[8,12,8,896]{3,2,1,0:T(8,128)(2,1)} %bitcast.6, f32[896]{0:T(1024)} %egain.1, bf16[896,1792]{1,0:T(8,128)(2,1)} %w_in.1, bf16[1792,896]{1,0:T(8,128)(2,1)} %w_out.1, ...), custom_call_target="tpu_custom_call" | custom-call | tf_op jit(solution)/shard_map/step/pallas_call | solution.py:718
  92.5 0.7 copy.19
  93.2 0.7 copy.20
  93.9 0.7 copy.21

commit v4 on v3

--- a/solution.py
+++ b/solution.py
@@ -21,8 +21,8 @@
 SM = pl.BlockSpec(memory_space=pltpu.SMEM)
 HB = pl.BlockSpec(memory_space=pltpu.HBM)
 BIG = 46000 * 1024
-FORE = (4, 2, 1)
-AFT = (2, 3, 2)
+FORE = (4, 3)
+AFT = (3, 4)
 
 
 def rcopy(src, dst, ssem, rsem, **where):
@@ -69,27 +69,24 @@
 def seq_exchange(n_seq, n, src, dst, send, recv, src_lanes=None):
     me = lax.axis_index("seq")
 
-    def piece(k, sending):
-        peer = lax.rem(me + k, n_seq) if sending else lax.rem(me + n_seq - k, n_seq)
-        at = me if sending else peer
-        if src_lanes is None:
-            a, b = src.at[peer, pl.ds(0, n)], dst.at[at, pl.ds(0, n)]
-        else:
-            a, b = src.at[peer, pl.ds(0, n), :, src_lanes], dst.at[at, pl.ds(0, n)]
-        return rcopy(a, b, send.at[peer], recv.at[at], seq=peer)
-
-    def run(sending, act):
+    def copy(at, to, count, peer):
+        a = src.at[pl.ds(at, count), pl.ds(0, n)]
+        if src_lanes is not None:
+            a = src.at[pl.ds(at, count), pl.ds(0, n), :, src_lanes]
+        return rcopy(a, dst.at[pl.ds(to, count), pl.ds(0, n)], send, recv, seq=peer)
+
+    def start():
         def go(k, carry):
-            act(piece(k, sending))
+            peer = lax.rem(me + k, n_seq)
+            copy(peer, me, 1, peer).start()
             return carry
 
         lax.fori_loop(1, n_seq, go, 0)
 
-    return (
-        lambda: run(True, lambda copy: copy.start()),
-        lambda: run(False, lambda copy: copy.wait_recv()),
-        lambda: run(True, lambda copy: copy.wait_send()),
-    )
+    def whole():
+        return copy(0, 0, n_seq - 1, lax.rem(me + 1, n_seq))
+
+    return start, lambda: whole().wait_recv(), lambda: whole().wait_send()
 
 
 def cuts(e, sizes):
@@ -102,12 +99,19 @@
     return out
 
 
-def loop(count, f):
+def loop(count, f, unroll=1):
     def go(i, carry):
         f(i)
         return carry
 
-    lax.fori_loop(0, count, go, 0)
+    lax.fori_loop(0, count, go, 0, unroll=unroll)
+
+
+def total_of(*parts):
+    out = parts[0].astype(F32)
+    for part in parts[1:]:
+        out = out + part.astype(F32)
+    return out.astype(BF16)
 
 
 def step_kernel(
@@ -163,7 +167,7 @@
         rows_s[d] = row
         name_s[d] = named
 
-    loop(n_seq, find)
+    loop(n_seq, find, 2)
 
     units = rows_dev * 2 * UNIT
     loads[0].wait()
@@ -184,7 +188,7 @@
     def stage_out(d):
         outg[d] = enc[rows_s[d]]
 
-    loop(n_seq, stage_out)
+    loop(n_seq, stage_out, 4)
     for (l0, w), recv in zip(fore, recvs):
         recv[me] = outg[me, :, :, l0:l0 + w]
     pl.semaphore_wait(barrier, greeted)
@@ -277,12 +281,10 @@
         ask[n][i][1]()
         l0, w = fore[i]
 
-        def pick(j):
-            slot = shards[lax.rem(j, K), me * per_dev + j // K]
+        for j in range(nb):
+            slot = shards[j % K, me * per_dev + j // K]
             for u in range(n):
                 full[j, 3 * x + n - 1 + u, :, l0:l0 + w] = recvs[i][slot, u]
-
-        loop(nb, pick)
         for copy in ring_copies(n, i)[:5]:
             copy.start()
 
@@ -292,6 +294,9 @@
         copies[5].start()
         ring_got(n, i, 1)
         copies[6].start()
+
+    def ring_share(n, i):
+        copies = ring_copies(n, i)
         ring_got(n, i, 2)
         copies[7].start()
         ring_got(n, i, 3)
@@ -327,12 +332,14 @@
         loop(turns, go)
 
     each(ring_open, 0)
+    each(ring_pass, 0)
     for i in range(1, len(fore)):
-        each(ring_pass, i - 1)
         each(ring_open, i)
+        each(ring_share, i - 1)
+        each(ring_pass, i)
         each(ring_close, i - 1)
         project(i - 1)
-    each(ring_pass, len(fore) - 1)
+    each(ring_share, len(fore) - 1)
     each(ring_close, len(fore) - 1)
     project(len(fore) - 1)
 
@@ -418,15 +425,9 @@
 
         def add(k):
             pair_copy(n, i, k, n).wait_recv()
-
-            def go(j):
-                for u in range(n):
-                    comb[k, j, u, :, l0:l0 + w] = (
-                        terms[j, 3 * k + n - 1 + u, :, l0:l0 + w].astype(F32)
-                        + sib[k, j, u, :, l0:l0 + w].astype(F32)
-                    ).astype(BF16)
-
-            loop(nb, go)
+            comb[k, :, 0:n, :, l0:l0 + w] = total_of(
+                terms[:, pl.ds(3 * k + n - 1, n), :, l0:l0 + w], sib[k, :, 0:n, :, l0:l0 + w]
+            )
 
         add(opp)
         for h in range(2):
@@ -440,15 +441,8 @@
         l0, w = aft[i]
         for h in range(2):
             relay_of(n, i, h).wait_recv()
-
-            def add(j, h=h):
-                for u in range(n):
-                    comb[toward[h], half * h + j, u, :, l0:l0 + w] = (
-                        comb[toward[h], half * h + j, u, :, l0:l0 + w].astype(F32)
-                        + relay[h, j, u, :, l0:l0 + w].astype(F32)
-                    ).astype(BF16)
-
-            loop(half, add)
+            at = (toward[h], slice(half * h, half * h + half), slice(0, n), slice(None), slice(l0, l0 + w))
+            comb[at] = total_of(comb[at], relay[h, :, 0:n, :, l0:l0 + w])
             final_of(n, i, h).start()
 
     def give_back(n, i):
@@ -457,22 +451,15 @@
             plain_of(n, i, h).wait_recv()
             final_of(n, i, h).wait_recv()
 
-        def add(j):
-            for u in range(n):
-                ge[j, u, :, l0:l0 + w] = (
-                    comb[x, j, u, :, l0:l0 + w].astype(F32)
-                    + last[0, j, u, :, l0:l0 + w].astype(F32)
-                    + last[1, j, u, :, l0:l0 + w].astype(F32)
-                ).astype(BF16)
-
-        loop(nb, add)
+        at = (slice(None), slice(0, n), slice(None), slice(l0, l0 + w))
+        ge[at] = total_of(comb[(x, *at)], last[(0, *at)], last[(1, *at)])
 
         def stage(s):
             spot = pick_s[s]
             for u in range(n):
                 back[i][s, u] = ge[spot, u, :, l0:l0 + w]
 
-        loop(n_seq, stage)
+        loop(n_seq, stage, 8)
         for u in range(n):
             got_back[i][me, u] = back[i][me, u]
         returns[n][i][0]()
@@ -613,7 +600,7 @@
     for i in range(m):
         terms_of(i)
         each(pair_start, i)
-    loop(n_seq, find_back)
+    loop(n_seq, find_back, 2)
     out_terms()
     out_open(0)
     each(reduce_pair, 0)
@@ -653,7 +640,7 @@
                 )
 
             sums = lax.fori_loop(
-                0, n_seq, add, tuple(jnp.zeros((UNIT, w), F32) for _ in range(rows_dev))
+                0, n_seq, add, tuple(jnp.zeros((UNIT, w), F32) for _ in range(rows_dev)), unroll=2
             )
             for r in range(rows_dev):
                 acc[r, u, :, l0:l0 + w] = sums[r]
@@ -759,16 +746,16 @@
             pltpu.SMEM((n_seq,), jnp.int32),
             pltpu.SMEM((n_seq,), jnp.int32),
             dma((9,)),
-            dma((nf, n_seq)),
-            dma((nf, n_seq)),
+            dma((nf,)),
+            dma((nf,)),
             dma((nf, 11)),
             dma((nf, 11)),
             dma((na, nx + 6)),
             dma((na, nx + 6)),
             dma((2, nx + 3)),
             dma((2, nx + 3)),
-            dma((na, n_seq)),
-            dma((na, n_seq)),
+            dma((na,)),
+            dma((na,)),
             dma((na,)),
             dma((na,)),
         ],

time: 94.8 us -> 80.1 us (0.84)
  Pallas kernels: 91.9 us -> 77.1 us
    pallas_call x1, Pallas kernels: 91.9 us -> 77.1 us  [step(): pl.pallas_call(functools.partial(step_kernel, dims), out_shape=(jax.Shape...]
where the time goes in v4:
time: 80.1 us; the launch traced here: 79.9 us
  Pallas kernels  77.1 us (96%)
  local copies, waits for them, and re-layouts  2.15 us (3%)
    pallas_call x1, Pallas kernels, step(): pl.pallas_call(functools.partial(step_kernel, dims), out_shape=(jax.Shape...  77.1 us
    unnamed x3, local copies, waits for them, and re-layouts  2.15 us

profile of v4, /device:TPU:1, one launch (start us, length us, event | category | flops | bytes accessed | tf_op | source)
XLA Modules:
  0.0 79.9 jit_solution(461824795635831205)
XLA Ops:
  0.6 77.1 %step.1 = (bf16[384,256]{1,0:T(8,128)(2,1)S(1)}, f32[384,256]{1,0:T(8,128)S(1)}, f32[12,8,896]{2,1,0:T(8,128)S(1)}) custom-call(s32[2,192]{1,0:T(2,128)} %bitcast.8, s32[2,192]{1,0:T(2,128)} %bitcast.9, bf16[8,12,8,896]{3,2,1,0:T(8,128)(2,1)} %bitcast.6, f32[896]{0:T(1024)} %egain.1, bf16[896,1792]{1,0:T(8,128)(2,1)} %w_in.1, bf16[1792,896]{1,0:T(8,128)(2,1)} %w_out.1, ...), custom_call_target="tpu_custom_call" | custom-call | tf_op jit(solution)/shard_map/step/pallas_call | solution.py:705
  77.8 0.7 copy.19
  78.5 0.7 copy.20
  79.2 0.7 copy.21
